TPU v7x, 128 devices: a whole 4x4x4 slice. The times are simulated.
128 devices in a mesh: layer: 4 (over z_hi, core), row: 32 (over x, y, z_lo).
Axes of the slice: x: 4, y: 4, z: 4 (z_hi: 2, z_lo: 2; z = z_hi * 2 + z_lo), core: 2. Of those that a mesh axis runs over, the one named last changes fastest.
Arguments:
- magnet: float32 [3, 4, 2048, 2048], P(None, 'layer', 'row'), may hold values from -6 to 6
- kernel: float32 [7, 6, 2048, 2048], P(None, None, ('layer', 'row')), may hold values from -1.8 to 1.8, as said below
Outputs:
- demag: float32 [3, 4, 2048, 2048], P(None, 'layer', 'row')
Inputs may be any that keep to these rules, and one draw needn't show every extreme that they name: With q' = -q mod 2048 and p' = -p mod 2048: parts 0, 1, 2 satisfy kernel[o, j, q', p] = kernel[o, j, q, p'] = kernel[o, j, q, p]; part 3 changes sign under either mirror; part 4 changes sign under p -> p' and keeps it under q -> q'; part 5 keeps its sign under p -> p' and changes it under q -> q'.
All inputs are finite; a program needn't handle non-finite values.
Results may differ from a plain program's by a relative error of at most 0.0001.
Values sent between devices are 32-bit elements; how exact they have to be, the bound alone decides.
No kernel may reach another device: no remote copies, remote signals or barrier semaphores. Data moves between devices by JAX's collectives and lax.ppermute only.
A program may use at most 256 MiB of HBM per device.

v0:
```python
import math

import jax
import jax.numpy as jnp
import numpy as np
from jax import lax
from jax.experimental import pallas as pl
from jax.experimental.pallas import tpu as pltpu
from jax.sharding import PartitionSpec as P

CELLS = 2048
COMPS = 3
LAYERS = 4
ROWS = 32
X_ROWS = 64
DEVICES = 128
PARTS = 6
OFFSETS = 7
OPS = OFFSETS * PARTS
FINE = 256
COARSE = 8
SLOT = COMPS * COARSE
LANES = 128
EXTRA = 16
P1_ROWS = LAYERS * COMPS * COARSE
P1_ALL = P1_ROWS + EXTRA

F32 = jnp.float32
BF16 = jnp.bfloat16


def halves(table):
    high = np.asarray(table, np.float32).astype(jnp.bfloat16)
    low = (np.asarray(table, np.float64) - high.astype(np.float64)).astype(np.float32).astype(jnp.bfloat16)
    return high, low


def second_digit():
    m = np.arange(DEVICES)
    return np.where(m < DEVICES // 2, 2 * m, 2 * DEVICES - 1 - 2 * m)


def fine_table():
    b = np.arange(FINE)
    k2 = second_digit()
    near = 2.0 * np.pi * (np.outer(b, k2) % FINE) / FINE
    far = 2.0 * np.pi * (np.outer(b, FINE - 1 - k2) % FINE) / FINE
    top = np.concatenate([np.cos(near), -np.sin(near), np.cos(far), np.sin(far)], axis=1)
    bottom = np.concatenate([np.sin(near), np.cos(near), np.sin(far), -np.cos(far)], axis=1)
    return np.concatenate([top, bottom], axis=0)


def closing_table():
    b = np.arange(FINE)
    k2 = second_digit()
    angle = 2.0 * np.pi * (np.outer(k2, b) % FINE) / FINE
    real = 2.0 * np.cos(angle)
    imag = -2.0 * np.sin(angle)
    real[0] = 1.0
    imag[0] = np.where(b % 2 == 0, 1.0, -1.0)
    return np.concatenate([real, imag], axis=0)


def y_twiddle(sign, scale):
    k = np.arange(1, 5)[:, None]
    b = np.arange(FINE)[None, :]
    angle = 2.0 * np.pi * k * b / CELLS
    table = scale * np.stack([np.cos(angle), sign * np.sin(angle)], axis=1)
    return table.reshape(8, FINE).astype(np.float32)


def lane_pair(coefficient):
    real = np.concatenate([coefficient.real, coefficient.real], axis=-1)
    imag = np.concatenate([-coefficient.imag, coefficient.imag], axis=-1)
    return real, imag


def x_twiddle(sign, scale):
    p1 = np.arange(ROWS)[:, None]
    t = np.arange(X_ROWS)[None, :]
    base = scale * np.exp(sign * 2.0j * np.pi * (p1 * t) / CELLS)
    side = np.where(p1 <= ROWS // 2, 1.0, -1.0) * (sign * 1.0j)
    kinds = []
    for kind in (1.0, 1.0j):
        first = lane_pair(kind * base)
        second = lane_pair(kind * base * side)
        kinds.append(np.stack(first + second, axis=1))
    return np.stack(kinds).astype(np.float32).reshape(2 * ROWS * 4, LANES)


def x_table(sign):
    index = np.arange(X_ROWS)
    angle = 2.0 * np.pi * (np.outer(index, index) % X_ROWS) / X_ROWS
    real = np.cos(angle)
    imag = sign * np.sin(angle)
    whole = np.block([[real, imag], [-imag, real]])
    high, low = halves(whole)
    line = np.concatenate([high, low], axis=1)
    return np.concatenate([line, line], axis=0)


def real_dft(values):
    n = len(values)
    if n == 1:
        return [values[0]], [None]
    if n == 2:
        return [values[0] + values[1], values[0] - values[1]], [None, None]
    even_c, even_s = real_dft(values[0::2])
    odd_c, odd_s = real_dft(values[1::2])
    half = n // 2
    quarter = n // 4
    cos_out = [None] * (half + 1)
    sin_out = [None] * (half + 1)
    for k in range(quarter + 1):
        if k == 0:
            cos_out[0] = even_c[0] + odd_c[0]
            cos_out[half] = even_c[0] - odd_c[0]
        elif k == quarter:
            cos_out[k] = even_c[k]
            sin_out[k] = odd_c[k]
        else:
            theta = 2.0 * math.pi * k / n
            cosine, sine = math.cos(theta), math.sin(theta)
            if 8 * k == n:
                real = cosine * (odd_c[k] - odd_s[k])
                imag = cosine * (odd_s[k] + odd_c[k])
            else:
                real = cosine * odd_c[k] - sine * odd_s[k]
                imag = cosine * odd_s[k] + sine * odd_c[k]
            cos_out[k] = even_c[k] + real
            sin_out[k] = even_s[k] + imag
            cos_out[half - k] = even_c[k] - real
            sin_out[half - k] = imag - even_s[k]
    return cos_out, sin_out


def real_sum(cos_in, sin_in, n):
    if n == 1:
        return [cos_in[0]]
    half = n // 2
    if n == 2:
        return [cos_in[0] + cos_in[1], cos_in[0] - cos_in[1]]
    quarter = n // 4
    even_c = [None] * (quarter + 1)
    even_s = [None] * (quarter + 1)
    odd_c = [None] * (quarter + 1)
    odd_s = [None] * (quarter + 1)
    even_c[0] = cos_in[0] + cos_in[half]
    odd_c[0] = cos_in[0] - cos_in[half]
    even_c[quarter] = cos_in[quarter]
    odd_c[quarter] = sin_in[quarter]
    for k in range(1, quarter):
        theta = 2.0 * math.pi * k / n
        cosine, sine = math.cos(theta), math.sin(theta)
        even_c[k] = cos_in[k] + cos_in[half - k]
        even_s[k] = sin_in[k] - sin_in[half - k]
        gap = cos_in[k] - cos_in[half - k]
        both = sin_in[k] + sin_in[half - k]
        if 8 * k == n:
            odd_c[k] = cosine * (gap + both)
            odd_s[k] = cosine * (both - gap)
        else:
            odd_c[k] = cosine * gap + sine * both
            odd_s[k] = cosine * both - sine * gap
    evens = real_sum(even_c, even_s, half)
    odds = real_sum(odd_c, odd_s, half)
    out = [None] * n
    out[0::2] = evens
    out[1::2] = odds
    return out


def split_pair(value):
    high = value.astype(BF16)
    low = (value - high.astype(F32)).astype(BF16)
    return high, low


def dot(left, right):
    return jnp.dot(left, right, preferred_element_type=F32)


def triple_dot(left, high, low):
    left_high, left_low = split_pair(left)
    return dot(left_high, high) + (dot(left_low, high) + dot(left_high, low))


def forward_y_kernel(x_ref, high_ref, low_ref, twiddle_ref, out_ref):
    root = math.sqrt(0.5)
    part = [x_ref[:, FINE * a : FINE * (a + 1)] for a in range(COARSE)]
    s04, d04 = part[0] + part[4], part[0] - part[4]
    s26, d26 = part[2] + part[6], part[2] - part[6]
    s15, d15 = part[1] + part[5], part[1] - part[5]
    s37, d37 = part[3] + part[7], part[3] - part[7]
    even, odd = s04 + s26, s15 + s37
    minus, plus = root * (d15 - d37), root * (d15 + d37)
    sums = [
        (even + odd, None),
        (d04 + minus, -(d26 + plus)),
        (s04 - s26, s37 - s15),
        (d04 - minus, d26 - plus),
        (even - odd, None),
    ]
    flat = out_ref.reshape(DEVICES * COARSE, LANES)
    lane = lax.broadcasted_iota(jnp.int32, (X_ROWS, LANES), 1)
    half = DEVICES // 2

    def emit(real, imag, k1):
        block = jnp.concatenate([real, imag], axis=0).T
        flat[pl.ds(k1, half, stride=COARSE), :] = block[:half]
        flat[pl.ds(half * COARSE + COARSE - 1 - k1, half, stride=COARSE), :] = block[half:]

    for k in range(5):
        real, imag = sums[k]
        if k > 0:
            cosine = twiddle_ref[2 * k - 2 : 2 * k - 1, :]
            sine = twiddle_ref[2 * k - 1 : 2 * k, :]
            if imag is None:
                real, imag = real * cosine, real * sine
            else:
                real, imag = real * cosine - imag * sine, real * sine + imag * cosine
        if k == 0:
            out = triple_dot(real, high_ref[:FINE, : 2 * LANES], low_ref[:FINE, : 2 * LANES])
            sign = 1.0 - 2.0 * (lax.broadcasted_iota(jnp.int32, (X_ROWS, FINE), 1) % 2).astype(F32)
            nyquist = jnp.sum(real * sign, axis=1, keepdims=True)
            emit(out[:, :LANES], jnp.where(lane == 0, nyquist, out[:, LANES:]), 0)
        elif k == 4:
            out = triple_dot(
                jnp.concatenate([real, imag], axis=1), high_ref[:, : 2 * LANES], low_ref[:, : 2 * LANES]
            )
            emit(out[:, :LANES], out[:, LANES:], 4)
        else:
            out = triple_dot(jnp.concatenate([real, imag], axis=1), high_ref[...], low_ref[...])
            emit(out[:, :LANES], out[:, LANES : 2 * LANES], k)
            emit(out[:, 2 * LANES : 3 * LANES], out[:, 3 * LANES :], COARSE - k)


def relayout_kernel(flag_ref, kernel_ref, out_ref, rows_ref, columns_ref):
    mirrored = flag_ref[0] > 0
    n_ops = kernel_ref.shape[0] // 16
    first = pl.program_id(0) * n_ops
    sub = lax.broadcasted_iota(jnp.int32, (COARSE, CELLS), 0)
    for op in range(n_ops):
        low = kernel_ref[16 * op : 16 * op + 8, :]
        high = kernel_ref[16 * op + 8 : 16 * op + 16, :]
        moved = jnp.where(sub < 7, pltpu.roll(low, 7, 0), pltpu.roll(high, 7, 0))
        part = (first + op) % PARTS
        odd = jnp.logical_or(part == 3, part == 5)
        sign = jnp.where(odd, -1.0, 1.0).astype(F32)
        rows_ref[8 * op : 8 * op + 8, :] = jnp.where(mirrored, moved * sign, low)
    for tile in range(CELLS // LANES):
        block = rows_ref[:, LANES * tile : LANES * (tile + 1)].T
        columns_ref[LANES * tile : LANES * (tile + 1), : 8 * n_ops] = block

    def step(p1, carry):
        column = columns_ref[pl.ds(p1, X_ROWS, stride=ROWS), :]
        both = jnp.concatenate([column, column], axis=0).T
        out_ref[p1] = both[: 8 * n_ops]
        return carry

    lax.fori_loop(0, ROWS, step, 0, unroll=4)


def spectral_kernel(
    x_ref,
    kernel_hbm,
    delta_ref,
    twiddle_ref,
    back_twiddle_ref,
    table_ref,
    back_table_ref,
    out_ref,
    kernel_ref,
    extra_ref,
    sums_ref,
    pair_ref,
    spec_ref,
    fix_ref,
    kernel_sem,
):
    fetch = pltpu.make_async_copy(kernel_hbm, kernel_ref, kernel_sem)
    fetch.start()
    half = ROWS // 2
    lane = lax.broadcasted_iota(jnp.int32, (ROWS, LANES), 1)

    extra_ref[...] = jnp.zeros_like(extra_ref)
    for layer in range(LAYERS):
        for comp in range(COMPS):
            line = x_ref[pl.ds(layer * ROWS * SLOT + comp * COARSE, ROWS, stride=SLOT), :]
            extra_ref[pl.ds(comp * LAYERS + layer, ROWS, stride=EXTRA), :] = jnp.where(lane < X_ROWS, 0.0, line)
    fix_ref[...] = jnp.zeros_like(fix_ref)

    def store_sums(values, place):
        cos_out, sin_out = real_dft(values)
        for k in range(half + 1):
            sums_ref[pl.ds(k * P1_ALL + place, COARSE), :] = cos_out[k]
        for k in range(1, half):
            sums_ref[pl.ds((half + k) * P1_ALL + place, COARSE), :] = sin_out[k]

    def over_rows(index, carry):
        layer = index // COMPS
        comp = index % COMPS
        base = layer * (ROWS * SLOT) + comp * COARSE
        base = pl.multiple_of(base, COARSE)
        values = [x_ref[pl.ds(base + r * SLOT, COARSE), :] for r in range(ROWS)]
        store_sums(values, pl.multiple_of(index * COARSE, COARSE))
        return carry

    lax.fori_loop(0, LAYERS * COMPS, over_rows, 0)
    for group in range(2):
        values = [extra_ref[r * EXTRA + group * 8 : r * EXTRA + group * 8 + 8, :] for r in range(ROWS)]
        store_sums(values, P1_ROWS + group * 8)

    def factors(ref, p1, kind):
        base = kind * (ROWS * 4) + p1 * 4
        return [ref[pl.ds(base + j, 1), :] for j in range(4)]

    def save_pair(row, value):
        high, low = split_pair(value)
        pair_ref[pl.ds(row, value.shape[0]), :LANES] = high
        pair_ref[pl.ds(row, value.shape[0]), LANES:] = low

    kinds = [1 if j % COMPS == 2 else 0 for j in range(LAYERS * COMPS)] + [0, 1]

    def blocks(ref, row, count):
        return [ref[pl.ds(row + COARSE * j, COARSE), :] for j in range(count)]

    def twist(k, p1_list, with_sin):
        cos_rows = blocks(sums_ref, pl.multiple_of(k * P1_ALL, COARSE), len(kinds))
        cos_swap = [pltpu.roll(v, X_ROWS, 1) for v in cos_rows]
        if with_sin:
            sin_rows = blocks(sums_ref, pl.multiple_of((half + k) * P1_ALL, COARSE), len(kinds))
            sin_swap = [pltpu.roll(v, X_ROWS, 1) for v in sin_rows]
        for p1 in p1_list:
            table = [factors(twiddle_ref, p1, kind) for kind in range(2)]
            out = []
            for j, kind in enumerate(kinds):
                f = table[kind]
                value = cos_rows[j] * f[0] + cos_swap[j] * f[1]
                if with_sin:
                    value = value + (sin_rows[j] * f[2] + sin_swap[j] * f[3])
                out.append(value)
            for j in range(0, len(kinds), 2):
                row = p1 * P1_ALL + COARSE * j
                save_pair(pl.multiple_of(row, 2 * COARSE), jnp.concatenate(out[j : j + 2], axis=0))

    twist(0, [0], False)
    twist(half, [half], False)

    def twist_step(k, carry):
        twist(k, [k, ROWS - k], True)
        return carry

    lax.fori_loop(1, half, twist_step, 0)

    def forward_dot(step, carry):
        rows = 4 * P1_ALL
        base = pl.multiple_of(step * rows, 2 * COARSE)
        both = dot(pair_ref[pl.ds(base, rows), :], table_ref[...])
        spec_ref[pl.ds(base, rows), :] = both[:, :LANES] + both[:, LANES:]
        return carry

    lax.fori_loop(0, ROWS // 4, forward_dot, 0)
    fetch.wait()

    def mix(spectra, coefficient):
        fields = []
        for target in range(LAYERS):
            total = [None, None, None]

            def add(comp, term):
                total[comp] = term if total[comp] is None else total[comp] + term

            for source in range(LAYERS):
                offset = target - source + LAYERS - 1
                k = [coefficient(offset * PARTS + j) for j in range(PARTS)]
                mx, my, mz = spectra[source]
                add(0, k[0] * mx + k[3] * my + k[4] * mz)
                add(1, k[3] * mx + k[1] * my + k[5] * mz)
                add(2, k[4] * mx + k[5] * my - k[2] * mz)
            fields.append(total)
        return fields

    def fix_step(group, carry):
        base = group * COARSE
        spectra = [
            [
                spec_ref[pl.ds(base * P1_ALL + P1_ROWS + comp * LAYERS + source, COARSE, stride=P1_ALL), :]
                for comp in range(COMPS)
            ]
            for source in range(LAYERS)
        ]

        def coefficient(op):
            return delta_ref[pl.ds(pl.multiple_of(op * ROWS + base, COARSE), COARSE), :]

        fields = mix(spectra, coefficient)
        for target in range(LAYERS):
            for comp in range(COMPS):
                row = base * P1_ROWS + (target * COMPS + comp) * COARSE
                fix_ref[pl.ds(row, COARSE, stride=P1_ROWS), :] = fields[target][comp]
        return carry

    lax.fori_loop(0, ROWS // COARSE, fix_step, 0)

    def mix_step(p1, carry):
        base = pl.multiple_of(p1 * P1_ALL, COARSE)
        lines = blocks(spec_ref, base, LAYERS * COMPS)
        spectra = [lines[COMPS * s : COMPS * s + COMPS] for s in range(LAYERS)]
        kernel_base = pl.multiple_of(p1 * (OPS * COARSE), COARSE)

        def coefficient(op):
            return kernel_ref[pl.ds(kernel_base + op * COARSE, COARSE), :]

        fields = mix(spectra, coefficient)
        flat = [fields[j // COMPS][j % COMPS] for j in range(LAYERS * COMPS)]
        row = pl.multiple_of(p1 * P1_ROWS, 2 * COARSE)
        fixes = blocks(fix_ref, row, LAYERS * COMPS)
        flat = [a + b for a, b in zip(flat, fixes)]
        for j in range(0, LAYERS * COMPS, 2):
            save_pair(row + COARSE * j, jnp.concatenate(flat[j : j + 2], axis=0))
        return carry

    lax.fori_loop(0, ROWS, mix_step, 0)

    def backward_dot(step, carry):
        rows = 4 * P1_ROWS
        base = pl.multiple_of(step * rows, 2 * COARSE)
        both = dot(pair_ref[pl.ds(base, rows), :], back_table_ref[...])
        spec_ref[pl.ds(base, rows), :] = both[:, :LANES] + both[:, LANES:]
        return carry

    lax.fori_loop(0, ROWS // 4, backward_dot, 0)

    count = LAYERS * COMPS

    def untwist_edge(p1, slot):
        table = [factors(back_twiddle_ref, p1, kind) for kind in range(2)]
        for j, value in enumerate(blocks(spec_ref, p1 * P1_ROWS, count)):
            f = table[kinds[j]]
            sums_ref[pl.ds(slot * P1_ROWS + COARSE * j, COARSE), :] = value * f[0] + pltpu.roll(value, X_ROWS, 1) * f[1]

    untwist_edge(0, 0)
    untwist_edge(half, half)

    def untwist_step(k, carry):
        near = [factors(back_twiddle_ref, k, kind) for kind in range(2)]
        far = [factors(back_twiddle_ref, ROWS - k, kind) for kind in range(2)]
        near_rows = blocks(spec_ref, pl.multiple_of(k * P1_ROWS, COARSE), count)
        far_rows = blocks(spec_ref, pl.multiple_of((ROWS - k) * P1_ROWS, COARSE), count)
        cos_base = pl.multiple_of(k * P1_ROWS, COARSE)
        sin_base = pl.multiple_of((half + k) * P1_ROWS, COARSE)
        for j in range(count):
            n, f = near[kinds[j]], far[kinds[j]]
            a, b = near_rows[j], far_rows[j]
            a_swap, b_swap = pltpu.roll(a, X_ROWS, 1), pltpu.roll(b, X_ROWS, 1)
            sums_ref[pl.ds(cos_base + COARSE * j, COARSE), :] = (a * n[0] + a_swap * n[1]) + (b * f[0] + b_swap * f[1])
            sums_ref[pl.ds(sin_base + COARSE * j, COARSE), :] = (a * n[2] + a_swap * n[3]) + (b * f[2] + b_swap * f[3])
        return carry

    lax.fori_loop(1, half, untwist_step, 0)

    def back_rows(index, carry):
        place = pl.multiple_of(index * COARSE, COARSE)
        cos_in = [sums_ref[pl.ds(k * P1_ROWS + place, COARSE), :] for k in range(half + 1)]
        sin_in = [None] + [sums_ref[pl.ds((half + k) * P1_ROWS + place, COARSE), :] for k in range(1, half)] + [None]
        values = real_sum(cos_in, sin_in, ROWS)
        layer = index // COMPS
        comp = index % COMPS
        base = pl.multiple_of(layer * (ROWS * SLOT) + comp * COARSE, COARSE)
        for r in range(ROWS):
            out_ref[pl.ds(base + r * SLOT, COARSE), :] = values[r]
        return carry

    lax.fori_loop(0, LAYERS * COMPS, back_rows, 0)


def inverse_y_kernel(x_ref, high_ref, low_ref, first_high_ref, first_low_ref, twiddle_ref, out_ref):
    flat = x_ref.reshape(DEVICES * COARSE, LANES)
    half = DEVICES // 2

    def take(k1):
        near = flat[pl.ds(k1, half, stride=COARSE), :]
        far = flat[pl.ds(half * COARSE + COARSE - 1 - k1, half, stride=COARSE), :]
        block = jnp.concatenate([near, far], axis=0).T
        return [block[:X_ROWS], block[X_ROWS:]]

    cos_in = [None] * 5
    sin_in = [None] * 5
    for k in range(5):
        if k == 0:
            left = jnp.concatenate(take(0), axis=1)
            cos_in[0] = triple_dot(left, first_high_ref[...], first_low_ref[...])
            continue
        cosine = twiddle_ref[2 * k - 2 : 2 * k - 1, :]
        sine = twiddle_ref[2 * k - 1 : 2 * k, :]
        if k == 4:
            left = jnp.concatenate(take(4), axis=1)
            both = triple_dot(left, high_ref[: 2 * LANES, :], low_ref[: 2 * LANES, :])
            cos_in[4] = both[:, :FINE] * cosine - both[:, FINE:] * sine
            continue
        left = jnp.concatenate(take(k) + take(COARSE - k), axis=1)
        both = triple_dot(left, high_ref[...], low_ref[...])
        cos_in[k] = both[:, :FINE] * cosine - both[:, FINE:] * sine
        sin_in[k] = -(both[:, :FINE] * sine + both[:, FINE:] * cosine)
    values = real_sum(cos_in, sin_in, COARSE)
    for a in range(COARSE):
        out_ref[:, FINE * a : FINE * (a + 1)] = values[a]


def whole(shape):
    rank = len(shape)
    return pl.BlockSpec(shape, lambda *_: (0,) * rank)


def params():
    return pltpu.CompilerParams(vmem_limit_bytes=48 * 1024 * 1024)


def forward_y(field):
    high, low = halves(fine_table())
    twiddle = y_twiddle(-1.0, 1.0)
    return pl.pallas_call(
        forward_y_kernel,
        grid=(COMPS,),
        in_specs=[
            pl.BlockSpec((X_ROWS, CELLS), lambda c: (c, 0)),
            whole(high.shape),
            whole(low.shape),
            whole(twiddle.shape),
        ],
        out_specs=pl.BlockSpec((DEVICES, COARSE, LANES), lambda c: (0, c, 0)),
        out_shape=jax.ShapeDtypeStruct((DEVICES, SLOT, LANES), F32),
        compiler_params=params(),
        name="forward_y",
    )(field, jnp.asarray(high), jnp.asarray(low), jnp.asarray(twiddle))


def relayout(kernel, flag):
    groups = 3
    rows = OPS // groups * 16
    out_rows = OPS // groups * COARSE
    return pl.pallas_call(
        relayout_kernel,
        grid=(groups,),
        in_specs=[
            pl.BlockSpec(memory_space=pltpu.SMEM),
            pl.BlockSpec((rows, CELLS), lambda g: (g, 0)),
        ],
        out_specs=pl.BlockSpec((ROWS, out_rows, LANES), lambda g: (0, g, 0)),
        out_shape=jax.ShapeDtypeStruct((ROWS, OPS * COARSE, LANES), F32),
        scratch_shapes=[pltpu.VMEM((out_rows, CELLS), F32), pltpu.VMEM((CELLS, LANES), F32)],
        compiler_params=params(),
        name="relayout",
    )(flag, kernel)


def spectral(lines, kernel, delta):
    twiddle = x_twiddle(-1.0, 1.0)
    back_twiddle = x_twiddle(1.0, -1.0 / (CELLS * CELLS))
    table = x_table(-1.0)
    back_table = x_table(1.0)
    total = DEVICES * SLOT
    return pl.pallas_call(
        spectral_kernel,
        in_specs=[
            whole((total, LANES)),
            pl.BlockSpec(memory_space=pl.ANY),
            whole(delta.shape),
            whole(twiddle.shape),
            whole(back_twiddle.shape),
            whole(table.shape),
            whole(back_table.shape),
        ],
        out_specs=whole((total, LANES)),
        grid=(1,),
        out_shape=jax.ShapeDtypeStruct((total, LANES), F32),
        scratch_shapes=[
            pltpu.VMEM((ROWS * OPS * COARSE, LANES), F32),
            pltpu.VMEM((ROWS * EXTRA, LANES), F32),
            pltpu.VMEM((ROWS * P1_ALL, LANES), F32),
            pltpu.VMEM((ROWS * P1_ALL, 2 * LANES), BF16),
            pltpu.VMEM((ROWS * P1_ALL, LANES), F32),
            pltpu.VMEM((ROWS * P1_ROWS, LANES), F32),
            pltpu.SemaphoreType.DMA,
        ],
        compiler_params=params(),
        name="spectral",
    )(
        lines,
        kernel,
        delta,
        jnp.asarray(twiddle),
        jnp.asarray(back_twiddle),
        jnp.asarray(table),
        jnp.asarray(back_table),
    )


def inverse_y(spectra):
    high, low = halves(fine_table().T)
    first_high, first_low = halves(closing_table())
    twiddle = y_twiddle(1.0, 2.0)
    return pl.pallas_call(
        inverse_y_kernel,
        grid=(COMPS,),
        in_specs=[
            pl.BlockSpec((DEVICES, COARSE, LANES), lambda c: (0, c, 0)),
            whole(high.shape),
            whole(low.shape),
            whole(first_high.shape),
            whole(first_low.shape),
            whole(twiddle.shape),
        ],
        out_specs=pl.BlockSpec((X_ROWS, CELLS), lambda c: (c, 0)),
        out_shape=jax.ShapeDtypeStruct((COMPS * X_ROWS, CELLS), F32),
        compiler_params=params(),
        name="inverse_y",
    )(
        spectra,
        jnp.asarray(high),
        jnp.asarray(low),
        jnp.asarray(first_high),
        jnp.asarray(first_low),
        jnp.asarray(twiddle),
    )


def local(magnet, kernel):
    axes = ("layer", "row")
    device = lax.axis_index(axes)
    field = magnet.reshape(COMPS * X_ROWS, CELLS)
    flag = (device >= DEVICES // 2).astype(jnp.int32).reshape(1)
    edge = kernel[:, :, 0, :].reshape(OPS, CELLS)
    middle = lax.ppermute(edge, axes, [(DEVICES // 2, 0)])
    sent = forward_y(field)
    got = lax.all_to_all(sent, axes, 0, 0, tiled=True)
    coefficient = relayout(kernel.reshape(OPS * 16, CELLS), flag)
    delta = jnp.where(device == 0, middle - edge, 0.0)
    delta = jnp.swapaxes(delta.reshape(OPS, X_ROWS, ROWS), 1, 2)
    delta = jnp.concatenate([delta, delta], axis=2).reshape(OPS * ROWS, LANES)
    fields = spectral(
        got.reshape(DEVICES * SLOT, LANES), coefficient.reshape(ROWS * OPS * COARSE, LANES), delta
    )
    back = lax.all_to_all(fields.reshape(DEVICES, SLOT, LANES), axes, 0, 0, tiled=True)
    result = inverse_y(back)
    return result.reshape(COMPS, 1, X_ROWS, CELLS)


def solution(mesh):
    in_specs = (P(None, "layer", "row", None), P(None, None, ("layer", "row"), None))
    out_specs = P(None, "layer", "row", None)
    return jax.shard_map(local, mesh=mesh, in_specs=in_specs, out_specs=out_specs, check_vma=False)
```

profile of v0, /device:TPU:1, one launch (start us, length us, event | category | flops | bytes accessed | tf_op | source)
XLA Modules:
  0.0 93.7 jit_solution(5522395004303115601)
XLA Ops:
  0.0 1.4 %copy-done.1 = f32[3,1,64,2048]{3,2,1,0:T(8,128)S(1)} copy-done((f32[3,1,64,2048]{3,2,1,0:T(8,128)S(1)}, f32[3,1,64,2048]{3,2,1,0:T(8,128)}, u32[]{:S(2)}) %copy-start.1) | copy-done | bytes 1572888
  1.4 1.0 %copy-done.4 = bf16[512,512]{1,0:T(8,128)(2,1)S(1)} copy-done((bf16[512,512]{1,0:T(8,128)(2,1)S(1)}, bf16[512,512]{1,0:T(8,128)(2,1)}, u32[]{:S(2)}) %copy-start.4) | copy-done | bytes 524312
  2.5 1.0 %copy-done.5 = bf16[512,512]{1,0:T(8,128)(2,1)S(1)} copy-done((bf16[512,512]{1,0:T(8,128)(2,1)S(1)}, bf16[512,512]{1,0:T(8,128)(2,1)}, u32[]{:S(2)}) %copy-start.5) | copy-done | bytes 524312
  3.5 0.7 copy-done.13
  4.2 4.6 %forward_y.1 = f32[128,24,128]{2,1,0:T(8,128)} custom-call(f32[192,2048]{1,0:T(8,128)S(1)} %bitcast.15, bf16[512,512]{1,0:T(8,128)(2,1)S(1)} %copy-done.5, bf16[512,512]{1,0:T(8,128)(2,1)S(1)} %copy-done.4, f32[8,256]{1,0:T(8,128)S(1)} %copy-done.13), custom_call_target="tpu_custom_call" | custom-call | tf_op jit(solution)/shard_map/forward_y/pallas_call | solution.py:523
  8.8 11.5 %all-to-all-start = ((f32[128,24,128]{2,1,0:T(8,128)}), f32[128,24,128]{2,1,0:T(8,128)S(1)}, u32[]{:S(2)}, u32[]{:S(2)}) async-start(f32[128,24,128]{2,1,0:T(8,128)} %forward_y.1), calls=%async_computation | async-start | bytes 3145728 | tf_op jit(solution)/shard_map/all_to_all | solution.py:637
  20.2 2.6 %slice_reduce_fusion = f32[7,6,2048]{2,1,0:T(8,128)S(1)} fusion(f32[7,6,16,2048]{3,2,1,0:T(8,128)} %param.15), kind=kLoop, calls=%fused_computation.2 | loop fusion | bytes 688128 | tf_op jit(solution)/shard_map/slice | solution.py:634
  22.9 0.1 reshape_squeeze.3
  22.9 0.7 collective-permute-start
  23.7 6.9 %relayout.1 = f32[32,336,128]{2,1,0:T(8,128)S(1)} custom-call(s32[1]{0:T(128)} %bitcast.2.flag_ref, f32[672,2048]{1,0:T(8,128)} %bitcast.16), custom_call_target="tpu_custom_call" | custom-call | tf_op jit(solution)/shard_map/relayout/pallas_call | solution.py:543
  30.6 2.4 %copy-done = f32[32,336,128]{2,1,0:T(8,128)} copy-done((f32[32,336,128]{2,1,0:T(8,128)}, f32[32,336,128]{2,1,0:T(8,128)S(1)}, u32[]{:S(2)}) %copy-start) | copy-done | bytes 5505048
  33.0 0.4 reshape.35
  33.5 0.0 copy-start.6
  33.5 0.0 copy-start.8
  33.5 0.0 copy-start.9
  33.5 1.3 %copy.18 = f32[42,32,64]{2,1,0:T(8,128)} copy(f32[42,32,64]{1,2,0:T(8,128)S(1)} %bitcast.17) | data formatting | bytes 688128 | tf_op jit(solution)/shard_map/transpose | solution.py:640
  34.8 1.6 %pad_maximum_fusion = f32[42,32,128]{2,1,0:T(8,128)S(1)} fusion(f32[42,32,64]{2,1,0:T(8,128)} %copy.18), kind=kLoop, calls=%fused_computation | loop fusion | flops 172032 | bytes 1032192 | tf_op jit(solution)/shard_map/concatenate | solution.py:641
  36.3 8.9 %all-to-all-done = f32[128,24,128]{2,1,0:T(8,128)S(1)} async-done(((f32[128,24,128]{2,1,0:T(8,128)}), f32[128,24,128]{2,1,0:T(8,128)S(1)}, u32[]{:S(2)}, u32[]{:S(2)}) %all-to-all-start) | async-done | bytes 1572896 | tf_op jit(solution)/shard_map/all_to_all | solution.py:637
  45.2 10.0 %spectral.1 = f32[3072,128]{1,0:T(8,128)S(1)} custom-call(f32[3072,128]{1,0:T(8,128)S(1)} %bitcast.12, f32[10752,128]{1,0:T(8,128)} %bitcast.11, f32[1344,128]{1,0:T(8,128)S(1)} %bitcast.14, f32[256,128]{1,0:T(8,128)S(1)} %copy-done.9, f32[256,128]{1,0:T(8,128)S(1)} %copy-done.8, bf16[256,256]{1,0:T(8,128)(2,1)S(1)} %copy-done.7, bf16[256,256]{1,0:T(8,128)(2,1)S(1)} %copy-done.6), custom_call_target="tpu_custom_call" | custom-call | tf_op jit(solution)/shard_map/spectral/pallas_call | solution.py:564
  55.3 0.0 copy-start.2
  55.3 0.0 copy-start.3
  55.3 0.0 copy-start.10
  55.3 33.5 %all_to_all.10.x_ref = f32[128,24,128]{2,1,0:T(8,128)S(1)} all-to-all(f32[128,24,128]{2,1,0:T(8,128)S(1)} %bitcast.13), channel_id=1, replica_groups=mesh['layer'=4,'row'=32] {'layer','row'}, dimensions={0} | all-to-all | bytes 3145728 | tf_op jit(solution)/shard_map/all_to_all | solution.py:645
  88.9 4.8 %inverse_y.1 = f32[192,2048]{1,0:T(8,128)} custom-call(f32[128,24,128]{2,1,0:T(8,128)S(1)} %all_to_all.10.x_ref, bf16[512,512]{1,0:T(8,128)(2,1)S(1)} %copy-done.3, bf16[512,512]{1,0:T(8,128)(2,1)S(1)} %copy-done.2, bf16[256,256]{1,0:T(8,128)(2,1)S(1)} %copy-done.11, bf16[256,256]{1,0:T(8,128)(2,1)S(1)} %copy-done.10, f32[8,256]{1,0:T(8,128)S(1)} %copy-done.12), custom_call_target="tpu_custom_call" | custom-call | tf_op jit(solution)/shard_map/inverse_y/pallas_call | solution.py:604
  (19 shorter events, 0.1 us)
Async XLA Ops:
  0.0 1.4 %copy-start.1 = (f32[3,1,64,2048]{3,2,1,0:T(8,128)S(1)}, f32[3,1,64,2048]{3,2,1,0:T(8,128)}, u32[]{:S(2)}) copy-start(f32[3,1,64,2048]{3,2,1,0:T(8,128)} %param.14) | copy-start | bytes 4718596
  1.4 1.0 %copy-start.4 = (bf16[512,512]{1,0:T(8,128)(2,1)S(1)}, bf16[512,512]{1,0:T(8,128)(2,1)}, u32[]{:S(2)}) copy-start(bf16[512,512]{1,0:T(8,128)(2,1)} %constant.42.clone.low_ref) | copy-start | bytes 1572868
  2.5 1.0 %copy-start.5 = (bf16[512,512]{1,0:T(8,128)(2,1)S(1)}, bf16[512,512]{1,0:T(8,128)(2,1)}, u32[]{:S(2)}) copy-start(bf16[512,512]{1,0:T(8,128)(2,1)} %constant.41.clone.high_ref) | copy-start | bytes 1572868
  3.5 0.7 copy-start.13
  8.8 36.5 %all-to-all-start = ((f32[128,24,128]{2,1,0:T(8,128)}), f32[128,24,128]{2,1,0:T(8,128)S(1)}, u32[]{:S(2)}, u32[]{:S(2)}) async-start(f32[128,24,128]{2,1,0:T(8,128)} %forward_y.1), calls=%async_computation | async-start | bytes 3145728 | tf_op jit(solution)/shard_map/all_to_all | solution.py:637
  22.9 10.0 %collective-permute-start = (f32[42,2048]{1,0:T(8,128)S(1)}, f32[42,2048]{1,0:T(8,128)S(1)}, u32[]{:S(2)}, u32[]{:S(2)}) collective-permute-start(f32[42,2048]{1,0:T(8,128)S(1)} %reshape_squeeze.3), channel_id=1, source_target_pairs={{64,0}} | collective-permute-start | bytes 1032200 | tf_op jit(solution)/shard_map/ppermute | solution.py:635
  30.6 2.4 %copy-start = (f32[32,336,128]{2,1,0:T(8,128)}, f32[32,336,128]{2,1,0:T(8,128)S(1)}, u32[]{:S(2)}) copy-start(f32[32,336,128]{2,1,0:T(8,128)S(1)} %relayout.1) | copy-start | bytes 16515076
  33.5 11.8 %copy-start.6 = (bf16[256,256]{1,0:T(8,128)(2,1)S(1)}, bf16[256,256]{1,0:T(8,128)(2,1)}, u32[]{:S(2)}) copy-start(bf16[256,256]{1,0:T(8,128)(2,1)} %constant.47.clone.back_table_ref) | copy-start | bytes 393220
  33.5 11.8 %copy-start.7 = (bf16[256,256]{1,0:T(8,128)(2,1)S(1)}, bf16[256,256]{1,0:T(8,128)(2,1)}, u32[]{:S(2)}) copy-start(bf16[256,256]{1,0:T(8,128)(2,1)} %constant.46.clone.table_ref) | copy-start | bytes 393220
  33.5 11.7 %copy-start.8 = (f32[256,128]{1,0:T(8,128)S(1)}, f32[256,128]{1,0:T(8,128)}, u32[]{:S(2)}) copy-start(f32[256,128]{1,0:T(8,128)} %constant.45.clone.back_twiddle_ref) | copy-start | bytes 393220
  33.5 11.7 %copy-start.9 = (f32[256,128]{1,0:T(8,128)S(1)}, f32[256,128]{1,0:T(8,128)}, u32[]{:S(2)}) copy-start(f32[256,128]{1,0:T(8,128)} %constant.44.clone.twiddle_ref) | copy-start | bytes 393220
  55.3 33.6 %copy-start.2 = (bf16[512,512]{1,0:T(8,128)(2,1)S(1)}, bf16[512,512]{1,0:T(8,128)(2,1)}, u32[]{:S(2)}) copy-start(bf16[512,512]{1,0:T(8,128)(2,1)} %constant.49.clone.low_ref) | copy-start | bytes 1572868
  55.3 33.6 %copy-start.3 = (bf16[512,512]{1,0:T(8,128)(2,1)S(1)}, bf16[512,512]{1,0:T(8,128)(2,1)}, u32[]{:S(2)}) copy-start(bf16[512,512]{1,0:T(8,128)(2,1)} %constant.48.clone.high_ref) | copy-start | bytes 1572868
  55.3 33.6 %copy-start.10 = (bf16[256,256]{1,0:T(8,128)(2,1)S(1)}, bf16[256,256]{1,0:T(8,128)(2,1)}, u32[]{:S(2)}) copy-start(bf16[256,256]{1,0:T(8,128)(2,1)} %constant.51.clone.first_low_ref) | copy-start | bytes 393220
  55.3 33.6 %copy-start.11 = (bf16[256,256]{1,0:T(8,128)(2,1)S(1)}, bf16[256,256]{1,0:T(8,128)(2,1)}, u32[]{:S(2)}) copy-start(bf16[256,256]{1,0:T(8,128)(2,1)} %constant.50.clone.first_high_ref) | copy-start | bytes 393220
  55.3 33.6 %copy-start.12 = (f32[8,256]{1,0:T(8,128)S(1)}, f32[8,256]{1,0:T(8,128)}, u32[]{:S(2)}) copy-start(f32[8,256]{1,0:T(8,128)} %constant.52.clone.twiddle_ref) | copy-start | bytes 24580
where the time goes:
time: 94.1 us; the launch traced here: 93.7 us
  blocking collectives  33.5 us (36%)
  Pallas kernels  26.3 us (28%)
  starting transfers between devices  12.2 us (13%)
  local copies, waits for them, and re-layouts  11 us (12%)
  waiting for transfers between devices  8.88 us (9%)
  other arithmetic  1.59 us (2%)
    all_to_all x1, blocking collectives, local(): lax.all_to_all(fields.reshape(DEVICES, SLOT, LANES), axes, 0, 0, tiled=True)  33.5 us
    all_to_all x1, starting transfers between devices, local(): got = lax.all_to_all(sent, axes, 0, 0, tiled=True)  11.5 us
    pallas_call x1, Pallas kernels, spectral(): pl.pallas_call(spectral_kernel, in_specs=[whole((total, LANES)), pl.Block...  10 us
    all_to_all x1, waiting for transfers between devices, local(): got = lax.all_to_all(sent, axes, 0, 0, tiled=True)  8.88 us
    pallas_call x1, Pallas kernels, relayout(): pl.pallas_call(relayout_kernel, grid=(groups,), in_specs=[pl.BlockSpec(me...  6.89 us
    unnamed x28, local copies, waits for them, and re-layouts  6.64 us
    pallas_call x1, Pallas kernels, inverse_y(): pl.pallas_call(inverse_y_kernel, grid=(COMPS,), in_specs=[pl.BlockSpec((D...  4.82 us
    pallas_call x1, Pallas kernels, forward_y(): pl.pallas_call(forward_y_kernel, grid=(COMPS,), in_specs=[pl.BlockSpec((X...  4.57 us
  transfers between devices with their start and end apart: 2, of which 1 were waited for; matrix products, arithmetic and copies ran while one was open for 6% of the time, Pallas kernels for 7%

commit v1 on v0

v1 whole, which is shorter than its diff:
```python
import math

import jax
import jax.numpy as jnp
import numpy as np
from jax import lax
from jax.experimental import pallas as pl
from jax.experimental.pallas import tpu as pltpu
from jax.sharding import PartitionSpec as P

CELLS = 2048
COMPS = 3
LAYERS = 4
ROWS = 32
X_ROWS = 64
DEVICES = 128
PARTS = 6
OFFSETS = 7
OPS = OFFSETS * PARTS
FINE = 128
COARSE = 16
OWNED = 8
SLOT = COMPS * OWNED
LANES = 128
EXTRA = 16
P1_ROWS = LAYERS * COMPS * OWNED
P1_ALL = P1_ROWS + EXTRA

F32 = jnp.float32
BF16 = jnp.bfloat16


def halves(table):
    high = np.asarray(table, np.float32).astype(jnp.bfloat16)
    low = (np.asarray(table, np.float64) - high.astype(np.float64)).astype(np.float32).astype(jnp.bfloat16)
    return high, low


def fine_table():
    index = np.arange(FINE)
    angle = 2.0 * np.pi * (np.outer(index, index) % FINE) / FINE
    return np.block([[np.cos(angle), -np.sin(angle)], [np.sin(angle), np.cos(angle)]])


def stacked(table):
    return np.concatenate(halves(table), axis=0)


def y_twiddle(sign, scale):
    k = np.arange(1, COARSE // 2 + 1)[:, None]
    b = np.arange(FINE)[None, :]
    angle = 2.0 * np.pi * k * b / CELLS
    table = scale * np.stack([np.cos(angle), sign * np.sin(angle)], axis=1)
    return table.reshape(COARSE, FINE).astype(np.float32)


def lane_pair(coefficient):
    real = np.concatenate([coefficient.real, coefficient.real], axis=-1)
    imag = np.concatenate([-coefficient.imag, coefficient.imag], axis=-1)
    return real, imag


def x_twiddle(sign, scale):
    p1 = np.arange(ROWS)[:, None]
    t = np.arange(X_ROWS)[None, :]
    base = scale * np.exp(sign * 2.0j * np.pi * (p1 * t) / CELLS)
    side = np.where(p1 <= ROWS // 2, 1.0, -1.0) * (sign * 1.0j)
    kinds = []
    for kind in (1.0, 1.0j):
        first = lane_pair(kind * base)
        second = lane_pair(kind * base * side)
        kinds.append(np.stack(first + second, axis=1))
    return np.stack(kinds).astype(np.float32).reshape(2 * ROWS * 4, LANES)


def x_table(sign):
    index = np.arange(X_ROWS)
    angle = 2.0 * np.pi * (np.outer(index, index) % X_ROWS) / X_ROWS
    real = np.cos(angle)
    imag = sign * np.sin(angle)
    whole = np.block([[real, imag], [-imag, real]])
    high, low = halves(whole)
    line = np.concatenate([high, low], axis=1)
    return np.concatenate([line, line], axis=0)


def real_dft(values):
    n = len(values)
    if n == 1:
        return [values[0]], [None]
    if n == 2:
        return [values[0] + values[1], values[0] - values[1]], [None, None]
    even_c, even_s = real_dft(values[0::2])
    odd_c, odd_s = real_dft(values[1::2])
    half = n // 2
    quarter = n // 4
    cos_out = [None] * (half + 1)
    sin_out = [None] * (half + 1)
    for k in range(quarter + 1):
        if k == 0:
            cos_out[0] = even_c[0] + odd_c[0]
            cos_out[half] = even_c[0] - odd_c[0]
        elif k == quarter:
            cos_out[k] = even_c[k]
            sin_out[k] = odd_c[k]
        else:
            theta = 2.0 * math.pi * k / n
            cosine, sine = math.cos(theta), math.sin(theta)
            if 8 * k == n:
                real = cosine * (odd_c[k] - odd_s[k])
                imag = cosine * (odd_s[k] + odd_c[k])
            else:
                real = cosine * odd_c[k] - sine * odd_s[k]
                imag = cosine * odd_s[k] + sine * odd_c[k]
            cos_out[k] = even_c[k] + real
            sin_out[k] = even_s[k] + imag
            cos_out[half - k] = even_c[k] - real
            sin_out[half - k] = imag - even_s[k]
    return cos_out, sin_out


def real_sum(cos_in, sin_in, n):
    if n == 1:
        return [cos_in[0]]
    half = n // 2
    if n == 2:
        return [cos_in[0] + cos_in[1], cos_in[0] - cos_in[1]]
    quarter = n // 4
    even_c = [None] * (quarter + 1)
    even_s = [None] * (quarter + 1)
    odd_c = [None] * (quarter + 1)
    odd_s = [None] * (quarter + 1)
    even_c[0] = cos_in[0] + cos_in[half]
    odd_c[0] = cos_in[0] - cos_in[half]
    even_c[quarter] = cos_in[quarter]
    odd_c[quarter] = sin_in[quarter]
    for k in range(1, quarter):
        theta = 2.0 * math.pi * k / n
        cosine, sine = math.cos(theta), math.sin(theta)
        even_c[k] = cos_in[k] + cos_in[half - k]
        even_s[k] = sin_in[k] - sin_in[half - k]
        gap = cos_in[k] - cos_in[half - k]
        both = sin_in[k] + sin_in[half - k]
        if 8 * k == n:
            odd_c[k] = cosine * (gap + both)
            odd_s[k] = cosine * (both - gap)
        else:
            odd_c[k] = cosine * gap + sine * both
            odd_s[k] = cosine * both - sine * gap
    evens = real_sum(even_c, even_s, half)
    odds = real_sum(odd_c, odd_s, half)
    out = [None] * n
    out[0::2] = evens
    out[1::2] = odds
    return out


def split_pair(value):
    high = value.astype(BF16)
    low = (value - high.astype(F32)).astype(BF16)
    return high, low


def dot(left, right):
    return jnp.dot(left, right, preferred_element_type=F32)


def triple_dot(high, low, table_ref):
    size = table_ref.shape[0] // 2
    table_high, table_low = table_ref[:size, :], table_ref[size:, :]
    left = jnp.concatenate([high, low, high], axis=1)
    return dot(left, jnp.concatenate([table_high, table_high, table_low], axis=0))


def slot_rows(comp, k1):
    half = DEVICES // 2
    near = pl.ds(comp * OWNED + k1, half, stride=SLOT)
    far = pl.ds(half * SLOT + comp * OWNED + k1 - 1, half, stride=SLOT)
    return near, far


def forward_y_kernel(x_ref, table_ref, twiddle_ref, out_ref, high_ref, low_ref):
    half = DEVICES // 2
    middle = COARSE // 2
    group = 16
    lane = lax.broadcasted_iota(jnp.int32, (X_ROWS, LANES), 1)
    alternate = 1.0 - 2.0 * (lax.broadcasted_iota(jnp.int32, (X_ROWS, FINE), 1) % 2).astype(F32)
    for comp in range(COMPS):
        base = comp * (middle + 1) * X_ROWS
        nyquist = []
        for g in range(X_ROWS // group):
            top = comp * X_ROWS + g * group
            parts = [x_ref[top : top + group, FINE * a : FINE * (a + 1)] for a in range(COARSE)]
            cos_out, sin_out = real_dft(parts)
            nyquist.append(jnp.sum(cos_out[0] * alternate[:group], axis=1, keepdims=True))
            for k in range(middle + 1):
                rows = slice(base + k * X_ROWS + g * group, base + k * X_ROWS + (g + 1) * group)
                real = cos_out[k]
                imag = None
                if k > 0:
                    cosine = twiddle_ref[2 * k - 2 : 2 * k - 1, :]
                    sine = twiddle_ref[2 * k - 1 : 2 * k, :]
                    if k == middle:
                        real, imag = real * cosine, real * sine
                    else:
                        real, imag = real * cosine + sin_out[k] * sine, real * sine - sin_out[k] * cosine
                high_ref[rows, :LANES], low_ref[rows, :LANES] = split_pair(real)
                if imag is None:
                    zero = jnp.zeros((group, LANES), BF16)
                    high_ref[rows, LANES:], low_ref[rows, LANES:] = zero, zero
                else:
                    high_ref[rows, LANES:], low_ref[rows, LANES:] = split_pair(imag)
        size = (middle + 1) * X_ROWS
        out = triple_dot(high_ref[base : base + size, :], low_ref[base : base + size, :], table_ref)

        def pick(k):
            rows = out[k * X_ROWS : (k + 1) * X_ROWS]
            return rows[:, :LANES], rows[:, LANES:]

        for k in range(middle):
            real, imag = pick(k)
            if k == 0:
                last_real, last_imag = pick(middle)
                imag = jnp.where(lane == 0, jnp.concatenate(nyquist, axis=0), imag)
                real = jnp.where(lane < half, real, last_real)
                imag = jnp.where(lane < half, imag, last_imag)
            block = jnp.concatenate([real, imag], axis=0).T
            near, far = slot_rows(comp, k)
            if k == 0:
                far = slot_rows(comp, middle)[1]
            out_ref[near, :] = block[:half]
            out_ref[far, :] = block[half:]


def relayout_kernel(flag_ref, kernel_ref, out_ref, rows_ref, columns_ref):
    shifted = flag_ref[0] > 0
    n_ops = kernel_ref.shape[0] // 16
    sub = lax.broadcasted_iota(jnp.int32, (OWNED, CELLS), 0)
    for op in range(n_ops):
        low = kernel_ref[16 * op : 16 * op + 8, :]
        high = kernel_ref[16 * op + 8 : 16 * op + 16, :]
        moved = jnp.where(sub < 7, pltpu.roll(low, 7, 0), pltpu.roll(high, 7, 0))
        rows_ref[8 * op : 8 * op + 8, :] = jnp.where(shifted, moved, low)
    for tile in range(CELLS // LANES):
        block = rows_ref[:, LANES * tile : LANES * (tile + 1)].T
        columns_ref[LANES * tile : LANES * (tile + 1), : 8 * n_ops] = block

    def step(p1, carry):
        column = columns_ref[pl.ds(p1, X_ROWS, stride=ROWS), :]
        both = jnp.concatenate([column, column], axis=0).T
        out_ref[p1] = both[: 8 * n_ops]
        return carry

    lax.fori_loop(0, ROWS, step, 0, unroll=4)


def spectral_kernel(
    x_ref,
    kernel_hbm,
    delta_ref,
    twiddle_ref,
    back_twiddle_ref,
    table_ref,
    back_table_ref,
    out_ref,
    kernel_ref,
    extra_ref,
    sums_ref,
    pair_ref,
    spec_ref,
    fix_ref,
    back_ref,
    kernel_sem,
):
    fetch = pltpu.make_async_copy(kernel_hbm, kernel_ref, kernel_sem)
    fetch.start()
    half = ROWS // 2
    lane = lax.broadcasted_iota(jnp.int32, (ROWS, LANES), 1)

    extra_ref[...] = jnp.zeros_like(extra_ref)
    for layer in range(LAYERS):
        for comp in range(COMPS):
            line = x_ref[pl.ds(layer * ROWS * SLOT + comp * OWNED, ROWS, stride=SLOT), :]
            extra_ref[pl.ds(comp * LAYERS + layer, ROWS, stride=EXTRA), :] = jnp.where(lane < X_ROWS, 0.0, line)
    fix_ref[...] = jnp.zeros_like(fix_ref)

    def store_sums(values, place):
        cos_out, sin_out = real_dft(values)
        for k in range(half + 1):
            sums_ref[pl.ds(k * P1_ALL + place, OWNED), :] = cos_out[k]
        for k in range(1, half):
            sums_ref[pl.ds((half + k) * P1_ALL + place, OWNED), :] = sin_out[k]

    def over_rows(index, carry):
        layer = index // COMPS
        comp = index % COMPS
        base = layer * (ROWS * SLOT) + comp * OWNED
        base = pl.multiple_of(base, OWNED)
        values = [x_ref[pl.ds(base + r * SLOT, OWNED), :] for r in range(ROWS)]
        store_sums(values, pl.multiple_of(index * OWNED, OWNED))
        return carry

    lax.fori_loop(0, LAYERS * COMPS, over_rows, 0)
    for group in range(2):
        values = [extra_ref[r * EXTRA + group * 8 : r * EXTRA + group * 8 + 8, :] for r in range(ROWS)]
        store_sums(values, P1_ROWS + group * 8)

    def factors(ref, p1, kind):
        base = kind * (ROWS * 4) + p1 * 4
        return [ref[pl.ds(base + j, 1), :] for j in range(4)]

    def save_pair(row, value):
        high, low = split_pair(value)
        pair_ref[pl.ds(row, value.shape[0]), :LANES] = high
        pair_ref[pl.ds(row, value.shape[0]), LANES:] = low

    kinds = [1 if j % COMPS == 2 else 0 for j in range(LAYERS * COMPS)] + [0, 1]

    def blocks(ref, row, count):
        return [ref[pl.ds(row + OWNED * j, OWNED), :] for j in range(count)]

    def twist(k, p1_list, with_sin):
        cos_rows = blocks(sums_ref, pl.multiple_of(k * P1_ALL, OWNED), len(kinds))
        cos_swap = [pltpu.roll(v, X_ROWS, 1) for v in cos_rows]
        if with_sin:
            sin_rows = blocks(sums_ref, pl.multiple_of((half + k) * P1_ALL, OWNED), len(kinds))
            sin_swap = [pltpu.roll(v, X_ROWS, 1) for v in sin_rows]
        for place, p1 in enumerate(p1_list):
            table = [factors(twiddle_ref, p1, kind) for kind in range(2)]
            out = []
            for j, kind in enumerate(kinds):
                f = table[kind]
                value = cos_rows[j] * f[0] + cos_swap[j] * f[1]
                if with_sin:
                    value = value + (sin_rows[j] * f[2] + sin_swap[j] * f[3])
                out.append(value)
            for j in range(0, len(kinds), 2):
                row = 2 * k * P1_ALL + place * P1_ALL + OWNED * j
                save_pair(pl.multiple_of(row, 2 * OWNED), jnp.concatenate(out[j : j + 2], axis=0))

    def forward_dot(k, first, second):
        rows = 2 * P1_ALL
        base = k * rows if isinstance(k, int) else pl.multiple_of(k * rows, 2 * OWNED)
        both = dot(pair_ref[pl.ds(base, rows), :], table_ref[...])
        whole_line = both[:, :LANES] + both[:, LANES:]
        spec_ref[pl.ds(first * P1_ALL, P1_ALL), :] = whole_line[:P1_ALL]
        spec_ref[pl.ds(second * P1_ALL, P1_ALL), :] = whole_line[P1_ALL:]

    twist(0, [0], False)
    cos_edge = blocks(sums_ref, half * P1_ALL, len(kinds))
    table = [factors(twiddle_ref, half, kind) for kind in range(2)]
    edge = [v * table[kind][0] + pltpu.roll(v, X_ROWS, 1) * table[kind][1] for v, kind in zip(cos_edge, kinds)]
    for j in range(0, len(kinds), 2):
        save_pair(P1_ALL + OWNED * j, jnp.concatenate(edge[j : j + 2], axis=0))
    forward_dot(0, 0, half)
    twist(1, [1, ROWS - 1], True)

    def twist_step(k, carry):
        forward_dot(k - 1, k - 1, ROWS + 1 - k)
        twist(k, [k, ROWS - k], True)
        return carry

    lax.fori_loop(2, half, twist_step, 0)
    forward_dot(half - 1, half - 1, half + 1)
    fetch.wait()

    def mix(spectra, coefficient):
        fields = []
        for target in range(LAYERS):
            total = [None, None, None]

            def add(comp, term):
                total[comp] = term if total[comp] is None else total[comp] + term

            for source in range(LAYERS):
                offset = target - source + LAYERS - 1
                k = [coefficient(offset * PARTS + j) for j in range(PARTS)]
                mx, my, mz = spectra[source]
                add(0, k[0] * mx + k[3] * my + k[4] * mz)
                add(1, k[3] * mx + k[1] * my + k[5] * mz)
                add(2, k[4] * mx + k[5] * my - k[2] * mz)
            fields.append(total)
        return fields

    def fix_step(group, carry):
        base = group * OWNED
        spectra = [
            [
                spec_ref[pl.ds(base * P1_ALL + P1_ROWS + comp * LAYERS + source, OWNED, stride=P1_ALL), :]
                for comp in range(COMPS)
            ]
            for source in range(LAYERS)
        ]

        def coefficient(op):
            return delta_ref[pl.ds(pl.multiple_of(op * ROWS + base, OWNED), OWNED), :]

        fields = mix(spectra, coefficient)
        for target in range(LAYERS):
            for comp in range(COMPS):
                row = base * P1_ROWS + (target * COMPS + comp) * OWNED
                fix_ref[pl.ds(row, OWNED, stride=P1_ROWS), :] = fields[target][comp]
        return carry

    lax.fori_loop(0, ROWS // OWNED, fix_step, 0)

    def mix_line(p1):
        lines = blocks(spec_ref, p1 * P1_ALL, LAYERS * COMPS)
        spectra = [lines[COMPS * s : COMPS * s + COMPS] for s in range(LAYERS)]
        kernel_base = p1 * (OPS * OWNED)

        def coefficient(op):
            return kernel_ref[pl.ds(kernel_base + op * OWNED, OWNED), :]

        fields = mix(spectra, coefficient)
        flat = [fields[j // COMPS][j % COMPS] for j in range(LAYERS * COMPS)]
        row = p1 * P1_ROWS
        fixes = blocks(fix_ref, row, LAYERS * COMPS)
        flat = [a + b for a, b in zip(flat, fixes)]
        for j in range(0, LAYERS * COMPS, 2):
            save_pair(row + OWNED * j, jnp.concatenate(flat[j : j + 2], axis=0))

    def backward_dot(p1, rows):
        both = dot(pair_ref[pl.ds(p1 * P1_ROWS, rows), :], back_table_ref[...])
        back_ref[pl.ds(p1 * P1_ROWS, rows), :] = both[:, :LANES] + both[:, LANES:]

    mix_line(0)
    mix_line(1)

    def mix_step(step, carry):
        p1 = pl.multiple_of(2 * step, 2)
        backward_dot(p1 - 2, 2 * P1_ROWS)
        mix_line(p1)
        mix_line(p1 + 1)
        return carry

    lax.fori_loop(1, half, mix_step, 0)
    backward_dot(ROWS - 2, 2 * P1_ROWS)

    count = LAYERS * COMPS

    def untwist_edge(p1, slot):
        table = [factors(back_twiddle_ref, p1, kind) for kind in range(2)]
        for j, value in enumerate(blocks(back_ref, p1 * P1_ROWS, count)):
            f = table[kinds[j]]
            sums_ref[pl.ds(slot * P1_ROWS + OWNED * j, OWNED), :] = value * f[0] + pltpu.roll(value, X_ROWS, 1) * f[1]

    untwist_edge(0, 0)
    untwist_edge(half, half)

    def untwist_step(k, carry):
        near = [factors(back_twiddle_ref, k, kind) for kind in range(2)]
        far = [factors(back_twiddle_ref, ROWS - k, kind) for kind in range(2)]
        near_rows = blocks(back_ref, pl.multiple_of(k * P1_ROWS, OWNED), count)
        far_rows = blocks(back_ref, pl.multiple_of((ROWS - k) * P1_ROWS, OWNED), count)
        cos_base = pl.multiple_of(k * P1_ROWS, OWNED)
        sin_base = pl.multiple_of((half + k) * P1_ROWS, OWNED)
        for j in range(count):
            n, f = near[kinds[j]], far[kinds[j]]
            a, b = near_rows[j], far_rows[j]
            a_swap, b_swap = pltpu.roll(a, X_ROWS, 1), pltpu.roll(b, X_ROWS, 1)
            sums_ref[pl.ds(cos_base + OWNED * j, OWNED), :] = (a * n[0] + a_swap * n[1]) + (b * f[0] + b_swap * f[1])
            sums_ref[pl.ds(sin_base + OWNED * j, OWNED), :] = (a * n[2] + a_swap * n[3]) + (b * f[2] + b_swap * f[3])
        return carry

    lax.fori_loop(1, half, untwist_step, 0)

    def back_rows(index, carry):
        place = pl.multiple_of(index * OWNED, OWNED)
        cos_in = [sums_ref[pl.ds(k * P1_ROWS + place, OWNED), :] for k in range(half + 1)]
        sin_in = [None] + [sums_ref[pl.ds((half + k) * P1_ROWS + place, OWNED), :] for k in range(1, half)] + [None]
        values = real_sum(cos_in, sin_in, ROWS)
        layer = index // COMPS
        comp = index % COMPS
        base = pl.multiple_of(layer * (ROWS * SLOT) + comp * OWNED, OWNED)
        for r in range(ROWS):
            out_ref[pl.ds(base + r * SLOT, OWNED), :] = values[r]
        return carry

    lax.fori_loop(0, LAYERS * COMPS, back_rows, 0)


def inverse_y_kernel(x_ref, table_ref, twiddle_ref, out_hbm, high_ref, low_ref, lines_ref, result_ref, sem):
    half = DEVICES // 2
    middle = COARSE // 2
    group = 8
    lane = lax.broadcasted_iota(jnp.int32, (X_ROWS, LANES), 1)
    alternate = 1.0 - 2.0 * (lax.broadcasted_iota(jnp.int32, (group, FINE), 1) % 2).astype(F32)
    copies = []
    for comp in range(COMPS):
        size = (middle + 1) * X_ROWS
        base = comp * size

        def put(k, real, imag):
            rows = slice(base + k * X_ROWS, base + (k + 1) * X_ROWS)
            high_ref[rows, :LANES], low_ref[rows, :LANES] = split_pair(real)
            high_ref[rows, LANES:], low_ref[rows, LANES:] = split_pair(imag)

        for k in range(middle):
            near, far = slot_rows(comp, k)
            if k == 0:
                far = slot_rows(comp, middle)[1]
            block = jnp.concatenate([x_ref[near, :], x_ref[far, :]], axis=0).T
            real, imag = block[:X_ROWS], block[X_ROWS:]
            if k == 0:
                nyquist = imag[:, :1]
                put(middle, jnp.where(lane < half, 0.0, real), jnp.where(lane < half, 0.0, imag))
                scale = jnp.where(lane < half, jnp.where(lane == 0, 0.5, 1.0), 0.0)
                real, imag = real * scale, imag * scale
            put(k, real, imag)
        lines_ref[base : base + size, :] = triple_dot(
            high_ref[base : base + size, :], low_ref[base : base + size, :], table_ref
        )
        for g in range(X_ROWS // group):
            cos_in = [None] * (middle + 1)
            sin_in = [None] * (middle + 1)
            for k in range(middle + 1):
                rows = slice(base + k * X_ROWS + g * group, base + k * X_ROWS + (g + 1) * group)
                real = lines_ref[rows, :LANES]
                if k == 0:
                    cos_in[0] = 2.0 * real + nyquist[g * group : (g + 1) * group] * alternate
                    continue
                imag = lines_ref[rows, LANES:]
                cosine = twiddle_ref[2 * k - 2 : 2 * k - 1, :]
                sine = twiddle_ref[2 * k - 1 : 2 * k, :]
                cos_in[k] = real * cosine - imag * sine
                if k < middle:
                    sin_in[k] = -(real * sine + imag * cosine)
            values = real_sum(cos_in, sin_in, COARSE)
            top = comp * X_ROWS + g * group
            for a in range(COARSE):
                result_ref[top : top + group, FINE * a : FINE * (a + 1)] = values[a]
        span = pl.ds(comp * X_ROWS, X_ROWS)
        copy = pltpu.make_async_copy(result_ref.at[span], out_hbm.at[span], sem.at[comp])
        copy.start()
        copies.append(copy)
    for copy in copies:
        copy.wait()


VMEM = pl.BlockSpec(memory_space=pltpu.VMEM)
HBM = pl.BlockSpec(memory_space=pl.ANY)
FINE_ROWS = COMPS * (COARSE // 2 + 1) * X_ROWS


def params():
    return pltpu.CompilerParams(vmem_limit_bytes=48 * 1024 * 1024)


def forward_y(field):
    return pl.pallas_call(
        forward_y_kernel,
        in_specs=[VMEM] * 3,
        out_specs=VMEM,
        out_shape=jax.ShapeDtypeStruct((DEVICES * SLOT, LANES), F32),
        scratch_shapes=[pltpu.VMEM((FINE_ROWS, 2 * LANES), BF16)] * 2,
        compiler_params=params(),
        name="forward_y",
    )(field, jnp.asarray(stacked(fine_table())), jnp.asarray(y_twiddle(-1.0, 1.0)))


def relayout(kernel, flag):
    groups = 3
    rows = OPS // groups * 16
    out_rows = OPS // groups * OWNED
    return pl.pallas_call(
        relayout_kernel,
        grid=(groups,),
        in_specs=[
            pl.BlockSpec(memory_space=pltpu.SMEM),
            pl.BlockSpec((rows, CELLS), lambda g: (g, 0)),
        ],
        out_specs=pl.BlockSpec((ROWS, out_rows, LANES), lambda g: (0, g, 0)),
        out_shape=jax.ShapeDtypeStruct((ROWS, OPS * OWNED, LANES), F32),
        scratch_shapes=[pltpu.VMEM((out_rows, CELLS), F32), pltpu.VMEM((CELLS, LANES), F32)],
        compiler_params=params(),
        name="relayout",
    )(flag, kernel)


def spectral(lines, kernel, delta):
    twiddle = x_twiddle(-1.0, 1.0)
    back_twiddle = x_twiddle(1.0, -1.0 / (CELLS * CELLS))
    return pl.pallas_call(
        spectral_kernel,
        in_specs=[VMEM, HBM] + [VMEM] * 5,
        out_specs=VMEM,
        out_shape=jax.ShapeDtypeStruct((DEVICES * SLOT, LANES), F32),
        scratch_shapes=[
            pltpu.VMEM((ROWS * OPS * OWNED, LANES), F32),
            pltpu.VMEM((ROWS * EXTRA, LANES), F32),
            pltpu.VMEM((ROWS * P1_ALL, LANES), F32),
            pltpu.VMEM((ROWS * P1_ALL, 2 * LANES), BF16),
            pltpu.VMEM((ROWS * P1_ALL, LANES), F32),
            pltpu.VMEM((ROWS * P1_ROWS, LANES), F32),
            pltpu.VMEM((ROWS * P1_ROWS, LANES), F32),
            pltpu.SemaphoreType.DMA,
        ],
        compiler_params=params(),
        name="spectral",
    )(
        lines,
        kernel,
        delta,
        jnp.asarray(twiddle),
        jnp.asarray(back_twiddle),
        jnp.asarray(x_table(-1.0)),
        jnp.asarray(x_table(1.0)),
    )


def inverse_y(spectra):
    rows = COMPS * X_ROWS
    return pl.pallas_call(
        inverse_y_kernel,
        in_specs=[VMEM] * 3,
        out_specs=HBM,
        out_shape=jax.ShapeDtypeStruct((rows, CELLS), F32),
        scratch_shapes=[
            pltpu.VMEM((FINE_ROWS, 2 * LANES), BF16),
            pltpu.VMEM((FINE_ROWS, 2 * LANES), BF16),
            pltpu.VMEM((FINE_ROWS, 2 * LANES), F32),
            pltpu.VMEM((rows, CELLS), F32),
            pltpu.SemaphoreType.DMA((COMPS,)),
        ],
        compiler_params=params(),
        name="inverse_y",
    )(spectra, jnp.asarray(stacked(fine_table().T)), jnp.asarray(y_twiddle(1.0, 2.0)))


def exchange(lines):
    moved = lax.all_to_all(lines.reshape(DEVICES, SLOT, LANES), ("layer", "row"), 0, 0, tiled=True)
    return moved.reshape(DEVICES * SLOT, LANES)


def local(magnet, kernel):
    axes = ("layer", "row")
    device = lax.axis_index(axes)
    field = magnet.reshape(COMPS * X_ROWS, CELLS)
    flag = (device >= DEVICES // 2).astype(jnp.int32).reshape(1)
    edge = kernel[:, :, 0, :].reshape(OPS, CELLS)
    middle = lax.ppermute(edge, axes, [(DEVICES // 2, 0)])
    sent, middle = lax.optimization_barrier((forward_y(field), middle))
    got = exchange(sent)
    coefficient = relayout(kernel.reshape(OPS * 16, CELLS), flag)
    delta = jnp.where(device == 0, middle - edge, 0.0)
    delta = jnp.swapaxes(delta.reshape(OPS, X_ROWS, ROWS), 1, 2)
    delta = jnp.concatenate([delta, delta], axis=2).reshape(OPS * ROWS, LANES)
    fields = spectral(got, coefficient.reshape(ROWS * OPS * OWNED, LANES), delta)
    result = inverse_y(exchange(fields))
    return result.reshape(COMPS, 1, X_ROWS, CELLS)


def solution(mesh):
    in_specs = (P(None, "layer", "row", None), P(None, None, ("layer", "row"), None))
    out_specs = P(None, "layer", "row", None)
    return jax.shard_map(local, mesh=mesh, in_specs=in_specs, out_specs=out_specs, check_vma=False)
```

time: 94.1 us -> 84.6 us (0.90)
  Pallas kernels: 26.3 us -> 21.1 us
  blocking collectives: 33.5 us -> 28.8 us
  waiting for transfers between devices: 8.88 us -> 12.5 us
  local copies, waits for them, and re-layouts: 11 us -> 7.95 us
    pallas_call x3, Pallas kernels: 19.4 us -> 14.3 us  [the longest x1 9.13 us: spectral(): pl.pallas_call(spectral_kernel, in_specs=[VMEM, HBM] + [VMEM] * 5, out_sp...]
    all_to_all x1, blocking collectives: 33.5 us -> 28.8 us  [exchange(): lax.all_to_all(lines.reshape(DEVICES, SLOT, LANES), ('layer', 'row'), 0,...]
    all_to_all x1, waiting for transfers between devices: 8.88 us -> 12.5 us  [exchange(): lax.all_to_all(lines.reshape(DEVICES, SLOT, LANES), ('layer', 'row'), 0,...]
    unnamed x28 -> x20, local copies, waits for them, and re-layouts: 6.64 us -> 3.41 us
  transfers between devices with their start and end apart: 2 -> 2, of which waited for: 1 -> 1; matrix products, arithmetic and copies ran while one was open for 6% -> 4% of each run, Pallas kernels for 7% -> 11%
where the time goes in v1:
time: 84.6 us; the launch traced here: 84.4 us
  blocking collectives  28.8 us (34%)
  Pallas kernels  21.1 us (25%)
  waiting for transfers between devices  12.5 us (15%)
  starting transfers between devices  12.2 us (14%)
  local copies, waits for them, and re-layouts  7.95 us (9%)
  other arithmetic  1.61 us (2%)
    all_to_all x1, blocking collectives, exchange(): lax.all_to_all(lines.reshape(DEVICES, SLOT, LANES), ('layer', 'row'), 0,...  28.8 us
    all_to_all x1, waiting for transfers between devices, exchange(): lax.all_to_all(lines.reshape(DEVICES, SLOT, LANES), ('layer', 'row'), 0,...  12.5 us
    all_to_all x1, starting transfers between devices, exchange(): lax.all_to_all(lines.reshape(DEVICES, SLOT, LANES), ('layer', 'row'), 0,...  11.5 us
    pallas_call x1, Pallas kernels, spectral(): pl.pallas_call(spectral_kernel, in_specs=[VMEM, HBM] + [VMEM] * 5, out_sp...  9.13 us
    pallas_call x1, Pallas kernels, relayout(): pl.pallas_call(relayout_kernel, grid=(groups,), in_specs=[pl.BlockSpec(me...  6.81 us
    unnamed x20, local copies, waits for them, and re-layouts  3.41 us
    pallas_call x1, Pallas kernels, forward_y(): pl.pallas_call(forward_y_kernel, in_specs=[VMEM] * 3, out_specs=VMEM, out...  2.82 us
    slice x1, local copies, waits for them, and re-layouts, local(): edge = kernel[:, :, 0, :].reshape(OPS, CELLS)  2.77 us
  transfers between devices with their start and end apart: 2, of which 1 were waited for; matrix products, arithmetic and copies ran while one was open for 4% of the time, Pallas kernels for 11%

profile of v1, /device:TPU:1, one launch (start us, length us, event | category | flops | bytes accessed | tf_op | source)
XLA Modules:
  0.0 84.4 jit_solution(2252947122022744678)
XLA Ops:
  0.0 2.8 %slice_reduce_fusion = f32[7,6,2048]{2,1,0:T(8,128)S(1)} fusion(f32[7,6,16,2048]{3,2,1,0:T(8,128)} %param.11), kind=kLoop, calls=%fused_computation.2 | loop fusion | bytes 688128 | tf_op jit(solution)/shard_map/slice | solution.py:641
  2.8 0.1 reshape_squeeze.3
  2.8 0.7 collective-permute-start
  3.6 0.0 copy-start.3
  3.6 0.9 %copy-done.3 = bf16[512,256]{1,0:T(8,128)(2,1)S(1)} copy-done((bf16[512,256]{1,0:T(8,128)(2,1)S(1)}, bf16[512,256]{1,0:T(8,128)(2,1)}, u32[]{:S(2)}) %copy-start.3) | copy-done | bytes 262168
  4.5 2.8 %forward_y.1 = f32[3072,128]{1,0:T(8,128)} custom-call(f32[192,2048]{1,0:T(8,128)S(1)} %bitcast.18, bf16[512,256]{1,0:T(8,128)(2,1)S(1)} %copy-done.3, f32[16,128]{1,0:T(8,128)S(1)} %copy-done.9), custom_call_target="tpu_custom_call" | custom-call | tf_op jit(solution)/shard_map/forward_y/pallas_call | solution.py:551
  7.3 0.0 collective-permute-done
  7.3 11.5 %all-to-all-start = ((f32[128,24,128]{2,1,0:T(8,128)}), f32[128,24,128]{2,1,0:T(8,128)S(1)}, u32[]{:S(2)}, u32[]{:S(2)}) async-start(f32[128,24,128]{2,1,0:T(8,128)} %bitcast.1), calls=%async_computation | async-start | bytes 3145728 | tf_op jit(solution)/shard_map/all_to_all | solution.py:632
  18.9 6.8 %relayout.1 = f32[32,336,128]{2,1,0:T(8,128)S(1)} custom-call(s32[1]{0:T(128)} %bitcast.3.flag_ref, f32[672,2048]{1,0:T(8,128)} %bitcast.19), custom_call_target="tpu_custom_call" | custom-call | tf_op jit(solution)/shard_map/relayout/pallas_call | solution.py:566
  25.7 2.4 %copy-done = f32[32,336,128]{2,1,0:T(8,128)} copy-done((f32[32,336,128]{2,1,0:T(8,128)}, f32[32,336,128]{2,1,0:T(8,128)S(1)}, u32[]{:S(2)}) %copy-start) | copy-done | bytes 5505048
  28.1 0.4 reshape.42
  28.6 0.0 copy-start.4
  28.6 0.0 copy-start.5
  28.6 0.0 copy-start.6
  28.6 0.0 copy-start.7
  28.6 1.3 %copy.14 = f32[42,32,64]{2,1,0:T(8,128)} copy(f32[42,32,64]{1,2,0:T(8,128)S(1)} %bitcast.20) | data formatting | bytes 688128 | tf_op jit(solution)/shard_map/transpose | solution.py:647
  29.9 1.6 %pad_maximum_fusion = f32[42,32,128]{2,1,0:T(8,128)S(1)} fusion(f32[42,32,64]{2,1,0:T(8,128)} %copy.14), kind=kLoop, calls=%fused_computation | loop fusion | flops 172032 | bytes 1032192 | tf_op jit(solution)/shard_map/concatenate | solution.py:648
  31.5 12.5 %all-to-all-done = f32[128,24,128]{2,1,0:T(8,128)S(1)} async-done(((f32[128,24,128]{2,1,0:T(8,128)}), f32[128,24,128]{2,1,0:T(8,128)S(1)}, u32[]{:S(2)}, u32[]{:S(2)}) %all-to-all-start) | async-done | bytes 1572896 | tf_op jit(solution)/shard_map/all_to_all | solution.py:632
  44.0 0.0 copy-done.4
  44.0 9.1 %spectral.1 = f32[3072,128]{1,0:T(8,128)S(1)} custom-call(f32[3072,128]{1,0:T(8,128)S(1)} %bitcast.14, f32[10752,128]{1,0:T(8,128)} %bitcast.13, f32[1344,128]{1,0:T(8,128)S(1)} %bitcast.17, f32[256,128]{1,0:T(8,128)S(1)} %copy-done.7, f32[256,128]{1,0:T(8,128)S(1)} %copy-done.6, bf16[256,256]{1,0:T(8,128)(2,1)S(1)} %copy-done.5, bf16[256,256]{1,0:T(8,128)(2,1)S(1)} %copy-done.4), custom_call_target="tpu_custom_call" | custom-call | tf_op jit(solution)/shard_map/spectral/pallas_call | solution.py:584
  53.1 0.0 copy-start.2
  53.1 0.0 copy-start.8
  53.1 28.8 %all_to_all.10 = f32[128,24,128]{2,1,0:T(8,128)S(1)} all-to-all(f32[128,24,128]{2,1,0:T(8,128)S(1)} %bitcast.15), channel_id=1, replica_groups=mesh['layer'=4,'row'=32] {'layer','row'}, dimensions={0} | all-to-all | bytes 3145728 | tf_op jit(solution)/shard_map/all_to_all | solution.py:632
  82.0 2.4 %inverse_y.1 = f32[192,2048]{1,0:T(8,128)} custom-call(f32[3072,128]{1,0:T(8,128)S(1)} %bitcast.16, bf16[512,256]{1,0:T(8,128)(2,1)S(1)} %copy-done.2, f32[16,128]{1,0:T(8,128)S(1)} %copy-done.8), custom_call_target="tpu_custom_call" | custom-call | tf_op jit(solution)/shard_map/inverse_y/pallas_call | solution.py:614
  (11 shorter events, 0.1 us)
Async XLA Ops:
  0.0 3.5 %copy-start.9 = (f32[16,128]{1,0:T(8,128)S(1)}, f32[16,128]{1,0:T(8,128)}, u32[]{:S(2)}) copy-start(f32[16,128]{1,0:T(8,128)} %constant.34.clone.twiddle_ref) | copy-start | bytes 24580
  0.0 3.5 %copy-start.1 = (f32[3,1,64,2048]{3,2,1,0:T(8,128)S(1)}, f32[3,1,64,2048]{3,2,1,0:T(8,128)}, u32[]{:S(2)}) copy-start(f32[3,1,64,2048]{3,2,1,0:T(8,128)} %param.10) | copy-start | bytes 4718596
  2.8 4.5 %collective-permute-start = (f32[42,2048]{1,0:T(8,128)S(1)}, f32[42,2048]{1,0:T(8,128)S(1)}, u32[]{:S(2)}, u32[]{:S(2)}) collective-permute-start(f32[42,2048]{1,0:T(8,128)S(1)} %reshape_squeeze.3), channel_id=1, source_target_pairs={{64,0}} | collective-permute-start | bytes 1032200 | tf_op jit(solution)/shard_map/ppermute | solution.py:642
  3.6 1.0 %copy-start.3 = (bf16[512,256]{1,0:T(8,128)(2,1)S(1)}, bf16[512,256]{1,0:T(8,128)(2,1)}, u32[]{:S(2)}) copy-start(bf16[512,256]{1,0:T(8,128)(2,1)} %constant.33.clone.table_ref) | copy-start | bytes 786436
  7.3 36.6 %all-to-all-start = ((f32[128,24,128]{2,1,0:T(8,128)}), f32[128,24,128]{2,1,0:T(8,128)S(1)}, u32[]{:S(2)}, u32[]{:S(2)}) async-start(f32[128,24,128]{2,1,0:T(8,128)} %bitcast.1), calls=%async_computation | async-start | bytes 3145728 | tf_op jit(solution)/shard_map/all_to_all | solution.py:632
  25.7 2.4 %copy-start = (f32[32,336,128]{2,1,0:T(8,128)}, f32[32,336,128]{2,1,0:T(8,128)S(1)}, u32[]{:S(2)}) copy-start(f32[32,336,128]{2,1,0:T(8,128)S(1)} %relayout.1) | copy-start | bytes 16515076
  28.6 15.4 %copy-start.4 = (bf16[256,256]{1,0:T(8,128)(2,1)S(1)}, bf16[256,256]{1,0:T(8,128)(2,1)}, u32[]{:S(2)}) copy-start(bf16[256,256]{1,0:T(8,128)(2,1)} %constant.38.clone.back_table_ref) | copy-start | bytes 393220
  28.6 15.4 %copy-start.5 = (bf16[256,256]{1,0:T(8,128)(2,1)S(1)}, bf16[256,256]{1,0:T(8,128)(2,1)}, u32[]{:S(2)}) copy-start(bf16[256,256]{1,0:T(8,128)(2,1)} %constant.37.clone.table_ref) | copy-start | bytes 393220
  28.6 15.3 %copy-start.6 = (f32[256,128]{1,0:T(8,128)S(1)}, f32[256,128]{1,0:T(8,128)}, u32[]{:S(2)}) copy-start(f32[256,128]{1,0:T(8,128)} %constant.36.clone.back_twiddle_ref) | copy-start | bytes 393220
  28.6 15.3 %copy-start.7 = (f32[256,128]{1,0:T(8,128)S(1)}, f32[256,128]{1,0:T(8,128)}, u32[]{:S(2)}) copy-start(f32[256,128]{1,0:T(8,128)} %constant.35.clone.twiddle_ref) | copy-start | bytes 393220
  53.1 28.9 %copy-start.2 = (bf16[512,256]{1,0:T(8,128)(2,1)S(1)}, bf16[512,256]{1,0:T(8,128)(2,1)}, u32[]{:S(2)}) copy-start(bf16[512,256]{1,0:T(8,128)(2,1)} %constant.39.clone.table_ref) | copy-start | bytes 786436
  53.1 28.9 %copy-start.8 = (f32[16,128]{1,0:T(8,128)S(1)}, f32[16,128]{1,0:T(8,128)}, u32[]{:S(2)}) copy-start(f32[16,128]{1,0:T(8,128)} %constant.40.clone.twiddle_ref) | copy-start | bytes 24580

commit v2 on v1

--- a/solution.py
+++ b/solution.py
@@ -7,6 +7,7 @@
 from jax.experimental import pallas as pl
 from jax.experimental.pallas import tpu as pltpu
 from jax.sharding import PartitionSpec as P
+
 
 CELLS = 2048
 COMPS = 3
@@ -179,7 +180,44 @@
     return near, far
 
 
-def forward_y_kernel(x_ref, table_ref, twiddle_ref, out_ref, high_ref, low_ref):
+def forward_y_kernel(
+    x_hbm,
+    table_hbm,
+    twiddle_hbm,
+    kernel_hbm,
+    out_hbm,
+    edge_hbm,
+    high_ref,
+    low_ref,
+    x_ref,
+    table_ref,
+    twiddle_ref,
+    tiles_ref,
+    out_ref,
+    edge_ref,
+    sem,
+    tiles_sem,
+):
+    blocks = [pl.ds(comp * X_ROWS, X_ROWS) for comp in range(COMPS)]
+    copies = [pltpu.make_async_copy(x_hbm.at[b], x_ref.at[b], sem.at[c]) for c, b in enumerate(blocks)]
+    tables = [
+        pltpu.make_async_copy(table_hbm, table_ref, sem.at[COMPS]),
+        pltpu.make_async_copy(twiddle_hbm, twiddle_ref, sem.at[COMPS + 1]),
+    ]
+    n_tiles = CELLS // LANES
+    edges = [
+        pltpu.make_async_copy(
+            kernel_hbm.at[:, pl.ds(0, OWNED), pl.ds(LANES * j, LANES)], tiles_ref.at[j], tiles_sem.at[j]
+        )
+        for j in range(n_tiles)
+    ]
+    copies[0].start()
+    for copy in tables + copies[1:] + edges:
+        copy.start()
+    for copy in tables:
+        copy.wait()
+    slots = out_ref.reshape(DEVICES, SLOT, LANES)
+    saves = []
     half = DEVICES // 2
     middle = COARSE // 2
     group = 16
@@ -188,6 +226,7 @@
     for comp in range(COMPS):
         base = comp * (middle + 1) * X_ROWS
         nyquist = []
+        copies[comp].wait()
         for g in range(X_ROWS // group):
             top = comp * X_ROWS + g * group
             parts = [x_ref[top : top + group, FINE * a : FINE * (a + 1)] for a in range(COARSE)]
@@ -230,6 +269,20 @@
                 far = slot_rows(comp, middle)[1]
             out_ref[near, :] = block[:half]
             out_ref[far, :] = block[half:]
+        lines = (slice(None), pl.ds(comp * OWNED, OWNED))
+        save = pltpu.make_async_copy(slots.at[lines], out_hbm.at[lines], sem.at[COMPS + 2 + comp])
+        save.start()
+        saves.append(save)
+        if comp == COMPS - 2:
+            flat = tiles_ref.reshape(n_tiles * OPS * OWNED, LANES)
+            for j in range(n_tiles):
+                edges[j].wait()
+                edge_ref[:, LANES * j : LANES * (j + 1)] = flat[pl.ds(j * OPS * OWNED, OPS, stride=OWNED), :]
+            save = pltpu.make_async_copy(edge_ref, edge_hbm, sem.at[2 * COMPS + 2])
+            save.start()
+            saves.append(save)
+    for save in saves:
+        save.wait()
 
 
 def relayout_kernel(flag_ref, kernel_ref, out_ref, rows_ref, columns_ref):
@@ -539,24 +592,40 @@
 
 
 VMEM = pl.BlockSpec(memory_space=pltpu.VMEM)
-HBM = pl.BlockSpec(memory_space=pl.ANY)
+HBM = pl.BlockSpec(memory_space=pltpu.HBM)
 FINE_ROWS = COMPS * (COARSE // 2 + 1) * X_ROWS
 
 
-def params():
-    return pltpu.CompilerParams(vmem_limit_bytes=48 * 1024 * 1024)
-
-
-def forward_y(field):
+def params(mebibytes):
+    return pltpu.CompilerParams(vmem_limit_bytes=mebibytes * 1024 * 1024)
+
+
+def forward_y(field, kernel):
+    table = stacked(fine_table())
+    twiddle = y_twiddle(-1.0, 1.0)
     return pl.pallas_call(
         forward_y_kernel,
-        in_specs=[VMEM] * 3,
-        out_specs=VMEM,
-        out_shape=jax.ShapeDtypeStruct((DEVICES * SLOT, LANES), F32),
-        scratch_shapes=[pltpu.VMEM((FINE_ROWS, 2 * LANES), BF16)] * 2,
-        compiler_params=params(),
+        in_specs=[HBM] * 4,
+        out_specs=[HBM, HBM],
+        out_shape=[
+            jax.ShapeDtypeStruct((DEVICES, SLOT, LANES), F32),
+            jax.ShapeDtypeStruct((OPS, CELLS), F32),
+        ],
+        scratch_shapes=[
+            pltpu.VMEM((FINE_ROWS, 2 * LANES), BF16),
+            pltpu.VMEM((FINE_ROWS, 2 * LANES), BF16),
+            pltpu.VMEM((COMPS * X_ROWS, CELLS), F32),
+            pltpu.VMEM(table.shape, BF16),
+            pltpu.VMEM(twiddle.shape, F32),
+            pltpu.VMEM((CELLS // LANES, OPS, OWNED, LANES), F32),
+            pltpu.VMEM((DEVICES * SLOT, LANES), F32),
+            pltpu.VMEM((OPS, CELLS), F32),
+            pltpu.SemaphoreType.DMA((2 * COMPS + 3,)),
+            pltpu.SemaphoreType.DMA((CELLS // LANES,)),
+        ],
+        compiler_params=params(63),
         name="forward_y",
-    )(field, jnp.asarray(stacked(fine_table())), jnp.asarray(y_twiddle(-1.0, 1.0)))
+    )(field, jnp.asarray(table), jnp.asarray(twiddle), kernel)
 
 
 def relayout(kernel, flag):
@@ -573,7 +642,7 @@
         out_specs=pl.BlockSpec((ROWS, out_rows, LANES), lambda g: (0, g, 0)),
         out_shape=jax.ShapeDtypeStruct((ROWS, OPS * OWNED, LANES), F32),
         scratch_shapes=[pltpu.VMEM((out_rows, CELLS), F32), pltpu.VMEM((CELLS, LANES), F32)],
-        compiler_params=params(),
+        compiler_params=params(48),
         name="relayout",
     )(flag, kernel)
 
@@ -596,7 +665,7 @@
             pltpu.VMEM((ROWS * P1_ROWS, LANES), F32),
             pltpu.SemaphoreType.DMA,
         ],
-        compiler_params=params(),
+        compiler_params=params(48),
         name="spectral",
     )(
         lines,
@@ -623,7 +692,7 @@
             pltpu.VMEM((rows, CELLS), F32),
             pltpu.SemaphoreType.DMA((COMPS,)),
         ],
-        compiler_params=params(),
+        compiler_params=params(20),
         name="inverse_y",
     )(spectra, jnp.asarray(stacked(fine_table().T)), jnp.asarray(y_twiddle(1.0, 2.0)))
 
@@ -638,9 +707,8 @@
     device = lax.axis_index(axes)
     field = magnet.reshape(COMPS * X_ROWS, CELLS)
     flag = (device >= DEVICES // 2).astype(jnp.int32).reshape(1)
-    edge = kernel[:, :, 0, :].reshape(OPS, CELLS)
+    sent, edge = forward_y(field, kernel.reshape(OPS, 16, CELLS))
     middle = lax.ppermute(edge, axes, [(DEVICES // 2, 0)])
-    sent, middle = lax.optimization_barrier((forward_y(field), middle))
     got = exchange(sent)
     coefficient = relayout(kernel.reshape(OPS * 16, CELLS), flag)
     delta = jnp.where(device == 0, middle - edge, 0.0)

time: 84.6 us -> 87 us (1.028)
  blocking collectives: 28.8 us -> 33.4 us
  Pallas kernels: 21.1 us -> 23.6 us
  local copies, waits for them, and re-layouts: 7.95 us -> 5.79 us
  other arithmetic: 1.61 us -> 0.3 us
  waiting for transfers between devices: 12.5 us -> 11.4 us
    all_to_all x1, blocking collectives: 28.8 us -> 33.4 us  [exchange(): lax.all_to_all(lines.reshape(DEVICES, SLOT, LANES), ('layer', 'row'), 0,...]
    slice x1 -> x0, local copies, waits for them, and re-layouts: 2.77 us -> none  [local(): edge = kernel[:, :, 0, :].reshape(OPS, CELLS)]
    pallas_call x1, Pallas kernels: 2.82 us -> 5.29 us  [forward_y(): pl.pallas_call(forward_y_kernel, in_specs=[HBM] * 4, out_specs=[HBM, HBM]...]
    concatenate x1, other arithmetic: 1.56 us -> 0.25 us  [local(): delta = jnp.concatenate([delta, delta], axis=2).reshape(OPS * ROWS, LANES)]
    all_to_all x1, waiting for transfers between devices: 12.5 us -> 11.4 us  [exchange(): lax.all_to_all(lines.reshape(DEVICES, SLOT, LANES), ('layer', 'row'), 0,...]
    reshape x1, local copies, waits for them, and re-layouts: 0.44 us -> 1.54 us  [local(): delta = jnp.swapaxes(delta.reshape(OPS, X_ROWS, ROWS), 1, 2)]
    unnamed x20 -> x16, local copies, waits for them, and re-layouts: 3.41 us -> 2.44 us
  transfers between devices with their start and end apart: 2 -> 2, of which waited for: 1 -> 1; matrix products, arithmetic and copies ran while one was open for 4% -> 4% of each run, Pallas kernels for 11% -> 8%
where the time goes in v2:
time: 87 us; the launch traced here: 86.7 us
  blocking collectives  33.4 us (38%)
  Pallas kernels  23.6 us (27%)
  starting transfers between devices  12.2 us (14%)
  waiting for transfers between devices  11.4 us (13%)
  local copies, waits for them, and re-layouts  5.79 us (7%)
    all_to_all x1, blocking collectives, exchange(): lax.all_to_all(lines.reshape(DEVICES, SLOT, LANES), ('layer', 'row'), 0,...  33.4 us
    all_to_all x1, starting transfers between devices, exchange(): lax.all_to_all(lines.reshape(DEVICES, SLOT, LANES), ('layer', 'row'), 0,...  11.5 us
    all_to_all x1, waiting for transfers between devices, exchange(): lax.all_to_all(lines.reshape(DEVICES, SLOT, LANES), ('layer', 'row'), 0,...  11.4 us
    pallas_call x1, Pallas kernels, spectral(): pl.pallas_call(spectral_kernel, in_specs=[VMEM, HBM] + [VMEM] * 5, out_sp...  9.13 us
    pallas_call x1, Pallas kernels, relayout(): pl.pallas_call(relayout_kernel, grid=(groups,), in_specs=[pl.BlockSpec(me...  6.81 us
    pallas_call x1, Pallas kernels, forward_y(): pl.pallas_call(forward_y_kernel, in_specs=[HBM] * 4, out_specs=[HBM, HBM]...  5.29 us
    unnamed x16, local copies, waits for them, and re-layouts  2.44 us
    pallas_call x1, Pallas kernels, inverse_y(): pl.pallas_call(inverse_y_kernel, in_specs=[VMEM] * 3, out_specs=HBM, out_...  2.37 us
  transfers between devices with their start and end apart: 2, of which 1 were waited for; matrix products, arithmetic and copies ran while one was open for 4% of the time, Pallas kernels for 8%

profile of v2, /device:TPU:1, one launch (start us, length us, event | category | flops | bytes accessed | tf_op | source)
XLA Modules:
  0.0 86.7 jit_solution(12174076991972056021)
XLA Ops:
  0.0 5.3 %forward_y.1 = (f32[128,24,128]{2,1,0:T(8,128)}, f32[42,2048]{1,0:T(8,128)}) custom-call(f32[192,2048]{1,0:T(8,128)} %bitcast.21, bf16[512,256]{1,0:T(8,128)(2,1)} %constant.33.clone.table_hbm, f32[16,128]{1,0:T(8,128)} %constant.34.clone.twiddle_hbm, f32[42,16,2048]{2,1,0:T(8,128)} %bitcast.18), custom_call_target="tpu_custom_call" | custom-call | tf_op jit(solution)/shard_map/forward_y/pallas_call | solution.py:606
  5.3 0.0 copy-start.7
  5.3 11.5 %all-to-all-start = ((f32[128,24,128]{2,1,0:T(8,128)}), f32[128,24,128]{2,1,0:T(8,128)S(1)}, u32[]{:S(2)}, u32[]{:S(2)}) async-start(f32[128,24,128]{2,1,0:T(8,128)} %get-tuple-element.7), calls=%async_computation | async-start | bytes 3145728 | tf_op jit(solution)/shard_map/all_to_all | solution.py:701
  16.8 0.0 copy-done.7
  16.8 0.7 collective-permute-start
  17.5 6.8 %relayout.1 = f32[32,336,128]{2,1,0:T(8,128)S(1)} custom-call(s32[1]{0:T(128)} %bitcast.3.flag_ref, f32[672,2048]{1,0:T(8,128)} %bitcast.19), custom_call_target="tpu_custom_call" | custom-call | tf_op jit(solution)/shard_map/relayout/pallas_call | solution.py:635
  24.3 0.0 copy-start
  24.3 2.4 %copy-done = f32[32,336,128]{2,1,0:T(8,128)} copy-done((f32[32,336,128]{2,1,0:T(8,128)}, f32[32,336,128]{2,1,0:T(8,128)S(1)}, u32[]{:S(2)}) %copy-start) | copy-done | bytes 5505048
  26.8 0.0 collective-permute-done
  26.8 1.5 %reshape.42 = f32[42,64,32]{2,1,0:T(8,128)} reshape(f32[42,2048]{1,0:T(8,128)S(1)} %subtract_select_fusion) | data formatting | bytes 688128 | tf_op jit(solution)/shard_map/reshape | solution.py:715
  28.4 1.8 %copy.15 = f32[42,32,64]{2,1,0:T(8,128)S(1)} copy(f32[42,32,64]{1,2,0:T(8,128)} %bitcast.20) | data formatting | bytes 688128 | tf_op jit(solution)/shard_map/transpose | solution.py:715
  30.2 0.3 pad_maximum_fusion
  30.4 11.4 %all-to-all-done = f32[128,24,128]{2,1,0:T(8,128)S(1)} async-done(((f32[128,24,128]{2,1,0:T(8,128)}), f32[128,24,128]{2,1,0:T(8,128)S(1)}, u32[]{:S(2)}, u32[]{:S(2)}) %all-to-all-start) | async-done | bytes 1572896 | tf_op jit(solution)/shard_map/all_to_all | solution.py:701
  41.8 0.0 copy-done.2
  41.8 0.0 copy-done.3
  41.8 0.0 copy-done.4
  41.8 0.0 copy-done.5
  41.8 9.1 %spectral.1 = f32[3072,128]{1,0:T(8,128)S(1)} custom-call(f32[3072,128]{1,0:T(8,128)S(1)} %bitcast.14, f32[10752,128]{1,0:T(8,128)} %bitcast.13, f32[1344,128]{1,0:T(8,128)S(1)} %bitcast.17, f32[256,128]{1,0:T(8,128)S(1)} %copy-done.5, f32[256,128]{1,0:T(8,128)S(1)} %copy-done.4, bf16[256,256]{1,0:T(8,128)(2,1)S(1)} %copy-done.3, bf16[256,256]{1,0:T(8,128)(2,1)S(1)} %copy-done.2), custom_call_target="tpu_custom_call" | custom-call | tf_op jit(solution)/shard_map/spectral/pallas_call | solution.py:653
  50.9 0.0 copy-start.1
  50.9 0.0 copy-start.6
  51.0 33.4 %all_to_all.10 = f32[128,24,128]{2,1,0:T(8,128)S(1)} all-to-all(f32[128,24,128]{2,1,0:T(8,128)S(1)} %bitcast.15), channel_id=1, replica_groups=mesh['layer'=4,'row'=32] {'layer','row'}, dimensions={0} | all-to-all | bytes 3145728 | tf_op jit(solution)/shard_map/all_to_all | solution.py:701
  84.4 0.0 copy-done.1
  84.4 0.0 copy-done.6
  84.4 2.4 %inverse_y.1 = f32[192,2048]{1,0:T(8,128)} custom-call(f32[3072,128]{1,0:T(8,128)S(1)} %bitcast.16, bf16[512,256]{1,0:T(8,128)(2,1)S(1)} %copy-done.1, f32[16,128]{1,0:T(8,128)S(1)} %copy-done.6), custom_call_target="tpu_custom_call" | custom-call | tf_op jit(solution)/shard_map/inverse_y/pallas_call | solution.py:683
  (5 shorter events, 0.1 us)
Async XLA Ops:
  5.3 11.5 %copy-start.7 = (f32[42,2048]{1,0:T(8,128)S(1)}, f32[42,2048]{1,0:T(8,128)}, u32[]{:S(2)}) copy-start(f32[42,2048]{1,0:T(8,128)} %get-tuple-element.8) | copy-start | bytes 1032196
  5.3 36.5 %all-to-all-start = ((f32[128,24,128]{2,1,0:T(8,128)}), f32[128,24,128]{2,1,0:T(8,128)S(1)}, u32[]{:S(2)}, u32[]{:S(2)}) async-start(f32[128,24,128]{2,1,0:T(8,128)} %get-tuple-element.7), calls=%async_computation | async-start | bytes 3145728 | tf_op jit(solution)/shard_map/all_to_all | solution.py:701
  16.8 9.9 %collective-permute-start = (f32[42,2048]{1,0:T(8,128)S(1)}, f32[42,2048]{1,0:T(8,128)S(1)}, u32[]{:S(2)}, u32[]{:S(2)}) collective-permute-start(f32[42,2048]{1,0:T(8,128)S(1)} %copy-done.7), channel_id=1, source_target_pairs={{64,0}} | collective-permute-start | bytes 1032200 | tf_op jit(solution)/shard_map/ppermute | solution.py:711
  24.3 2.4 %copy-start = (f32[32,336,128]{2,1,0:T(8,128)}, f32[32,336,128]{2,1,0:T(8,128)S(1)}, u32[]{:S(2)}) copy-start(f32[32,336,128]{2,1,0:T(8,128)S(1)} %relayout.1) | copy-start | bytes 16515076
  28.3 13.4 %copy-start.2 = (bf16[256,256]{1,0:T(8,128)(2,1)S(1)}, bf16[256,256]{1,0:T(8,128)(2,1)}, u32[]{:S(2)}) copy-start(bf16[256,256]{1,0:T(8,128)(2,1)} %constant.38.clone.back_table_ref) | copy-start | bytes 393220
  28.3 13.4 %copy-start.3 = (bf16[256,256]{1,0:T(8,128)(2,1)S(1)}, bf16[256,256]{1,0:T(8,128)(2,1)}, u32[]{:S(2)}) copy-start(bf16[256,256]{1,0:T(8,128)(2,1)} %constant.37.clone.table_ref) | copy-start | bytes 393220
  28.4 13.4 %copy-start.4 = (f32[256,128]{1,0:T(8,128)S(1)}, f32[256,128]{1,0:T(8,128)}, u32[]{:S(2)}) copy-start(f32[256,128]{1,0:T(8,128)} %constant.36.clone.back_twiddle_ref) | copy-start | bytes 393220
  28.4 13.4 %copy-start.5 = (f32[256,128]{1,0:T(8,128)S(1)}, f32[256,128]{1,0:T(8,128)}, u32[]{:S(2)}) copy-start(f32[256,128]{1,0:T(8,128)} %constant.35.clone.twiddle_ref) | copy-start | bytes 393220
  50.9 33.4 %copy-start.1 = (bf16[512,256]{1,0:T(8,128)(2,1)S(1)}, bf16[512,256]{1,0:T(8,128)(2,1)}, u32[]{:S(2)}) copy-start(bf16[512,256]{1,0:T(8,128)(2,1)} %constant.39.clone.table_ref) | copy-start | bytes 786436
  50.9 33.4 %copy-start.6 = (f32[16,128]{1,0:T(8,128)S(1)}, f32[16,128]{1,0:T(8,128)}, u32[]{:S(2)}) copy-start(f32[16,128]{1,0:T(8,128)} %constant.40.clone.twiddle_ref) | copy-start | bytes 24580

commit v3 on v1

--- a/solution.py
+++ b/solution.py
@@ -7,6 +7,7 @@
 from jax.experimental import pallas as pl
 from jax.experimental.pallas import tpu as pltpu
 from jax.sharding import PartitionSpec as P
+
 
 CELLS = 2048
 COMPS = 3
@@ -179,7 +180,33 @@
     return near, far
 
 
-def forward_y_kernel(x_ref, table_ref, twiddle_ref, out_ref, high_ref, low_ref):
+EDGE_PARTS = 4
+EDGES = OFFSETS * EDGE_PARTS
+
+
+def edge_kernel(kernel_hbm, out_ref, tiles_ref, sem):
+    n_tiles = CELLS // LANES
+    copies = []
+    for j in range(n_tiles):
+        lanes = pl.ds(LANES * j, LANES)
+        for i, (source, target) in enumerate([((0, 3), (0, 3)), ((4, 1), (3, 1))]):
+            copy = pltpu.make_async_copy(
+                kernel_hbm.at[:, pl.ds(*source), pl.ds(0, OWNED), lanes],
+                tiles_ref.at[j, :, pl.ds(*target)],
+                sem.at[j, i],
+            )
+            copy.start()
+            copies.append(copy)
+    flat = tiles_ref.reshape(n_tiles * EDGES * OWNED, LANES)
+    for j in range(n_tiles):
+        copies[2 * j].wait()
+        copies[2 * j + 1].wait()
+        out_ref[:, LANES * j : LANES * (j + 1)] = flat[pl.ds(j * EDGES * OWNED, EDGES, stride=OWNED), :]
+
+
+def forward_y_kernel(x_ref, table_ref, twiddle_ref, out_hbm, high_ref, low_ref, out_ref, sem):
+    slots = out_ref.reshape(DEVICES, SLOT, LANES)
+    saves = []
     half = DEVICES // 2
     middle = COARSE // 2
     group = 16
@@ -230,6 +257,12 @@
                 far = slot_rows(comp, middle)[1]
             out_ref[near, :] = block[:half]
             out_ref[far, :] = block[half:]
+        lines = (slice(None), pl.ds(comp * OWNED, OWNED))
+        save = pltpu.make_async_copy(slots.at[lines], out_hbm.at[lines], sem.at[comp])
+        save.start()
+        saves.append(save)
+    for save in saves:
+        save.wait()
 
 
 def relayout_kernel(flag_ref, kernel_ref, out_ref, rows_ref, columns_ref):
@@ -364,7 +397,7 @@
     forward_dot(half - 1, half - 1, half + 1)
     fetch.wait()
 
-    def mix(spectra, coefficient):
+    def mix(spectra, coefficient, edge=False):
         fields = []
         for target in range(LAYERS):
             total = [None, None, None]
@@ -374,8 +407,14 @@
 
             for source in range(LAYERS):
                 offset = target - source + LAYERS - 1
+                mx, my, mz = spectra[source]
+                if edge:
+                    k = [coefficient(offset * EDGE_PARTS + j) for j in range(EDGE_PARTS)]
+                    add(0, k[0] * mx + k[3] * mz)
+                    add(1, k[1] * my)
+                    add(2, k[3] * mx - k[2] * mz)
+                    continue
                 k = [coefficient(offset * PARTS + j) for j in range(PARTS)]
-                mx, my, mz = spectra[source]
                 add(0, k[0] * mx + k[3] * my + k[4] * mz)
                 add(1, k[3] * mx + k[1] * my + k[5] * mz)
                 add(2, k[4] * mx + k[5] * my - k[2] * mz)
@@ -395,7 +434,7 @@
         def coefficient(op):
             return delta_ref[pl.ds(pl.multiple_of(op * ROWS + base, OWNED), OWNED), :]
 
-        fields = mix(spectra, coefficient)
+        fields = mix(spectra, coefficient, edge=True)
         for target in range(LAYERS):
             for comp in range(COMPS):
                 row = base * P1_ROWS + (target * COMPS + comp) * OWNED
@@ -539,24 +578,46 @@
 
 
 VMEM = pl.BlockSpec(memory_space=pltpu.VMEM)
-HBM = pl.BlockSpec(memory_space=pl.ANY)
+HBM = pl.BlockSpec(memory_space=pltpu.HBM)
 FINE_ROWS = COMPS * (COARSE // 2 + 1) * X_ROWS
 
 
-def params():
-    return pltpu.CompilerParams(vmem_limit_bytes=48 * 1024 * 1024)
+def params(mebibytes):
+    return pltpu.CompilerParams(vmem_limit_bytes=mebibytes * 1024 * 1024)
+
+
+def edge_lines(kernel):
+    return pl.pallas_call(
+        edge_kernel,
+        in_specs=[HBM],
+        out_specs=VMEM,
+        out_shape=jax.ShapeDtypeStruct((EDGES, CELLS), F32),
+        scratch_shapes=[
+            pltpu.VMEM((CELLS // LANES, OFFSETS, EDGE_PARTS, OWNED, LANES), F32),
+            pltpu.SemaphoreType.DMA((CELLS // LANES, 2)),
+        ],
+        compiler_params=params(58),
+        name="edge_lines",
+    )(kernel)
 
 
 def forward_y(field):
+    table = stacked(fine_table())
+    twiddle = y_twiddle(-1.0, 1.0)
     return pl.pallas_call(
         forward_y_kernel,
         in_specs=[VMEM] * 3,
-        out_specs=VMEM,
-        out_shape=jax.ShapeDtypeStruct((DEVICES * SLOT, LANES), F32),
-        scratch_shapes=[pltpu.VMEM((FINE_ROWS, 2 * LANES), BF16)] * 2,
-        compiler_params=params(),
+        out_specs=HBM,
+        out_shape=jax.ShapeDtypeStruct((DEVICES, SLOT, LANES), F32),
+        scratch_shapes=[
+            pltpu.VMEM((FINE_ROWS, 2 * LANES), BF16),
+            pltpu.VMEM((FINE_ROWS, 2 * LANES), BF16),
+            pltpu.VMEM((DEVICES * SLOT, LANES), F32),
+            pltpu.SemaphoreType.DMA((COMPS,)),
+        ],
+        compiler_params=params(48),
         name="forward_y",
-    )(field, jnp.asarray(stacked(fine_table())), jnp.asarray(y_twiddle(-1.0, 1.0)))
+    )(field, jnp.asarray(table), jnp.asarray(twiddle))
 
 
 def relayout(kernel, flag):
@@ -573,7 +634,7 @@
         out_specs=pl.BlockSpec((ROWS, out_rows, LANES), lambda g: (0, g, 0)),
         out_shape=jax.ShapeDtypeStruct((ROWS, OPS * OWNED, LANES), F32),
         scratch_shapes=[pltpu.VMEM((out_rows, CELLS), F32), pltpu.VMEM((CELLS, LANES), F32)],
-        compiler_params=params(),
+        compiler_params=params(48),
         name="relayout",
     )(flag, kernel)
 
@@ -596,7 +657,7 @@
             pltpu.VMEM((ROWS * P1_ROWS, LANES), F32),
             pltpu.SemaphoreType.DMA,
         ],
-        compiler_params=params(),
+        compiler_params=params(48),
         name="spectral",
     )(
         lines,
@@ -623,7 +684,7 @@
             pltpu.VMEM((rows, CELLS), F32),
             pltpu.SemaphoreType.DMA((COMPS,)),
         ],
-        compiler_params=params(),
+        compiler_params=params(20),
         name="inverse_y",
     )(spectra, jnp.asarray(stacked(fine_table().T)), jnp.asarray(y_twiddle(1.0, 2.0)))
 
@@ -638,14 +699,14 @@
     device = lax.axis_index(axes)
     field = magnet.reshape(COMPS * X_ROWS, CELLS)
     flag = (device >= DEVICES // 2).astype(jnp.int32).reshape(1)
-    edge = kernel[:, :, 0, :].reshape(OPS, CELLS)
+    edge = edge_lines(kernel)
     middle = lax.ppermute(edge, axes, [(DEVICES // 2, 0)])
-    sent, middle = lax.optimization_barrier((forward_y(field), middle))
+    sent = forward_y(field)
     got = exchange(sent)
     coefficient = relayout(kernel.reshape(OPS * 16, CELLS), flag)
     delta = jnp.where(device == 0, middle - edge, 0.0)
-    delta = jnp.swapaxes(delta.reshape(OPS, X_ROWS, ROWS), 1, 2)
-    delta = jnp.concatenate([delta, delta], axis=2).reshape(OPS * ROWS, LANES)
+    delta = jnp.swapaxes(delta.reshape(EDGES, X_ROWS, ROWS), 1, 2)
+    delta = jnp.concatenate([delta, delta], axis=2).reshape(EDGES * ROWS, LANES)
     fields = spectral(got, coefficient.reshape(ROWS * OPS * OWNED, LANES), delta)
     result = inverse_y(exchange(fields))
     return result.reshape(COMPS, 1, X_ROWS, CELLS)

time: 84.6 us -> 83.8 us (level)
  Pallas kernels: 21.1 us -> 23.5 us
  local copies, waits for them, and re-layouts: 7.95 us -> 6.09 us
  other arithmetic: 1.61 us -> 0.23 us
  waiting for transfers between devices: 12.5 us -> 11.5 us
  blocking collectives: 28.8 us -> 29.7 us
    slice x1 -> x0, local copies, waits for them, and re-layouts: 2.77 us -> none  [local(): edge = kernel[:, :, 0, :].reshape(OPS, CELLS)]
    pallas_call x1 -> x2, Pallas kernels: 2.82 us -> 5.17 us  [the longest x1 2.59 us: forward_y(): pl.pallas_call(forward_y_kernel, in_specs=[VMEM] * 3, out_specs=HBM, out_...]
    unnamed x20 -> x22, local copies, waits for them, and re-layouts: 3.41 us -> 5.5 us
    concatenate x1, other arithmetic: 1.56 us -> 0.19 us  [local(): delta = jnp.concatenate([delta, delta], axis=2).reshape(EDGES * ROWS, LANES)]
    transpose x1, local copies, waits for them, and re-layouts: 1.27 us -> 0.29 us  [local(): delta = jnp.swapaxes(delta.reshape(EDGES, X_ROWS, ROWS), 1, 2)]
    all_to_all x1, waiting for transfers between devices: 12.5 us -> 11.5 us  [exchange(): lax.all_to_all(lines.reshape(DEVICES, SLOT, LANES), ('layer', 'row'), 0,...]
    all_to_all x1, blocking collectives: 28.8 us -> 29.7 us  [exchange(): lax.all_to_all(lines.reshape(DEVICES, SLOT, LANES), ('layer', 'row'), 0,...]
  transfers between devices with their start and end apart: 2 -> 2, of which waited for: 1 -> 1; matrix products, arithmetic and copies ran while one was open for 4% -> 1% of each run, Pallas kernels for 11% -> 11%
where the time goes in v3:
time: 83.8 us; the launch traced here: 83.4 us
  blocking collectives  29.7 us (35%)
  Pallas kernels  23.5 us (28%)
  starting transfers between devices  12.2 us (15%)
  waiting for transfers between devices  11.5 us (14%)
  local copies, waits for them, and re-layouts  6.09 us (7%)
    all_to_all x1, blocking collectives, exchange(): lax.all_to_all(lines.reshape(DEVICES, SLOT, LANES), ('layer', 'row'), 0,...  29.7 us
    all_to_all x1, waiting for transfers between devices, exchange(): lax.all_to_all(lines.reshape(DEVICES, SLOT, LANES), ('layer', 'row'), 0,...  11.5 us
    all_to_all x1, starting transfers between devices, exchange(): lax.all_to_all(lines.reshape(DEVICES, SLOT, LANES), ('layer', 'row'), 0,...  11.5 us
    pallas_call x1, Pallas kernels, spectral(): pl.pallas_call(spectral_kernel, in_specs=[VMEM, HBM] + [VMEM] * 5, out_sp...  9.11 us
    pallas_call x1, Pallas kernels, relayout(): pl.pallas_call(relayout_kernel, grid=(groups,), in_specs=[pl.BlockSpec(me...  6.85 us
    unnamed x22, local copies, waits for them, and re-layouts  5.5 us
    pallas_call x1, Pallas kernels, forward_y(): pl.pallas_call(forward_y_kernel, in_specs=[VMEM] * 3, out_specs=HBM, out_...  2.59 us
    pallas_call x1, Pallas kernels, edge_lines(): pl.pallas_call(edge_kernel, in_specs=[HBM], out_specs=VMEM, out_shape=jax...  2.57 us
  transfers between devices with their start and end apart: 2, of which 1 were waited for; matrix products, arithmetic and copies ran while one was open for 1% of the time, Pallas kernels for 11%

profile of v3, /device:TPU:1, one launch (start us, length us, event | category | flops | bytes accessed | tf_op | source)
XLA Modules:
  0.0 83.4 jit_solution(13101934276713190334)
XLA Ops:
  0.0 1.4 %copy-done.1 = f32[3,1,64,2048]{3,2,1,0:T(8,128)S(1)} copy-done((f32[3,1,64,2048]{3,2,1,0:T(8,128)S(1)}, f32[3,1,64,2048]{3,2,1,0:T(8,128)}, u32[]{:S(2)}) %copy-start.1) | copy-done | bytes 1572888
  1.4 0.9 %copy-done.3 = bf16[512,256]{1,0:T(8,128)(2,1)S(1)} copy-done((bf16[512,256]{1,0:T(8,128)(2,1)S(1)}, bf16[512,256]{1,0:T(8,128)(2,1)}, u32[]{:S(2)}) %copy-start.3) | copy-done | bytes 262168
  2.4 0.7 copy-done.9
  3.1 2.6 %forward_y.1 = f32[128,24,128]{2,1,0:T(8,128)} custom-call(f32[192,2048]{1,0:T(8,128)S(1)} %bitcast.17, bf16[512,256]{1,0:T(8,128)(2,1)S(1)} %copy-done.3, f32[16,128]{1,0:T(8,128)S(1)} %copy-done.9), custom_call_target="tpu_custom_call" | custom-call | tf_op jit(solution)/shard_map/forward_y/pallas_call | solution.py:607
  5.7 11.5 %all-to-all-start = ((f32[128,24,128]{2,1,0:T(8,128)}), f32[128,24,128]{2,1,0:T(8,128)S(1)}, u32[]{:S(2)}, u32[]{:S(2)}) async-start(f32[128,24,128]{2,1,0:T(8,128)} %forward_y.1), calls=%async_computation | async-start | bytes 3145728 | tf_op jit(solution)/shard_map/all_to_all | solution.py:693
  17.2 2.6 %edge_lines.1 = f32[28,2048]{1,0:T(8,128)} custom-call(f32[7,6,16,2048]{3,2,1,0:T(8,128)} %kernel_hbm.1), custom_call_target="tpu_custom_call" | custom-call | tf_op jit(solution)/shard_map/edge_lines/pallas_call | solution.py:590
  19.7 0.7 collective-permute-start
  20.4 6.8 %relayout.1 = f32[32,336,128]{2,1,0:T(8,128)S(1)} custom-call(s32[1]{0:T(128)} %bitcast.2.flag_ref, f32[672,2048]{1,0:T(8,128)} %bitcast.18), custom_call_target="tpu_custom_call" | custom-call | tf_op jit(solution)/shard_map/relayout/pallas_call | solution.py:627
  27.3 2.4 %copy-done = f32[32,336,128]{2,1,0:T(8,128)} copy-done((f32[32,336,128]{2,1,0:T(8,128)}, f32[32,336,128]{2,1,0:T(8,128)S(1)}, u32[]{:S(2)}) %copy-start) | copy-done | bytes 5505048
  29.7 0.0 collective-permute-done
  29.7 0.0 copy-done.10
  29.8 0.0 copy-start.4
  29.8 0.0 copy-start.5
  29.8 0.0 copy-start.6
  29.8 0.0 copy-start.7
  29.8 0.3 reshape.38
  30.1 0.3 copy.15
  30.4 0.2 pad_maximum_fusion
  30.6 11.5 %all-to-all-done = f32[128,24,128]{2,1,0:T(8,128)S(1)} async-done(((f32[128,24,128]{2,1,0:T(8,128)}), f32[128,24,128]{2,1,0:T(8,128)S(1)}, u32[]{:S(2)}, u32[]{:S(2)}) %all-to-all-start) | async-done | bytes 1572896 | tf_op jit(solution)/shard_map/all_to_all | solution.py:693
  42.1 9.1 %spectral.1 = f32[3072,128]{1,0:T(8,128)S(1)} custom-call(f32[3072,128]{1,0:T(8,128)S(1)} %bitcast.13, f32[10752,128]{1,0:T(8,128)} %bitcast.12, f32[896,128]{1,0:T(8,128)S(1)} %bitcast.16, f32[256,128]{1,0:T(8,128)S(1)} %copy-done.7, f32[256,128]{1,0:T(8,128)S(1)} %copy-done.6, bf16[256,256]{1,0:T(8,128)(2,1)S(1)} %copy-done.5, bf16[256,256]{1,0:T(8,128)(2,1)S(1)} %copy-done.4), custom_call_target="tpu_custom_call" | custom-call | tf_op jit(solution)/shard_map/spectral/pallas_call | solution.py:645
  51.3 0.0 copy-start.2
  51.3 0.0 copy-start.8
  51.3 29.7 %all_to_all.10 = f32[128,24,128]{2,1,0:T(8,128)S(1)} all-to-all(f32[128,24,128]{2,1,0:T(8,128)S(1)} %bitcast.14), channel_id=1, replica_groups=mesh['layer'=4,'row'=32] {'layer','row'}, dimensions={0} | all-to-all | bytes 3145728 | tf_op jit(solution)/shard_map/all_to_all | solution.py:693
  81.0 2.4 %inverse_y.1 = f32[192,2048]{1,0:T(8,128)} custom-call(f32[3072,128]{1,0:T(8,128)S(1)} %bitcast.15, bf16[512,256]{1,0:T(8,128)(2,1)S(1)} %copy-done.2, f32[16,128]{1,0:T(8,128)S(1)} %copy-done.8), custom_call_target="tpu_custom_call" | custom-call | tf_op jit(solution)/shard_map/inverse_y/pallas_call | solution.py:675
  (12 shorter events, 0.1 us)
Async XLA Ops:
  0.0 1.4 %copy-start.1 = (f32[3,1,64,2048]{3,2,1,0:T(8,128)S(1)}, f32[3,1,64,2048]{3,2,1,0:T(8,128)}, u32[]{:S(2)}) copy-start(f32[3,1,64,2048]{3,2,1,0:T(8,128)} %param.10) | copy-start | bytes 4718596
  1.4 0.9 %copy-start.3 = (bf16[512,256]{1,0:T(8,128)(2,1)S(1)}, bf16[512,256]{1,0:T(8,128)(2,1)}, u32[]{:S(2)}) copy-start(bf16[512,256]{1,0:T(8,128)(2,1)} %constant.33.clone.table_ref) | copy-start | bytes 786436
  2.4 0.7 copy-start.9
  5.7 36.5 %all-to-all-start = ((f32[128,24,128]{2,1,0:T(8,128)}), f32[128,24,128]{2,1,0:T(8,128)S(1)}, u32[]{:S(2)}, u32[]{:S(2)}) async-start(f32[128,24,128]{2,1,0:T(8,128)} %forward_y.1), calls=%async_computation | async-start | bytes 3145728 | tf_op jit(solution)/shard_map/all_to_all | solution.py:693
  19.7 10.0 %collective-permute-start = (f32[28,2048]{1,0:T(8,128)}, f32[28,2048]{1,0:T(8,128)S(1)}, u32[]{:S(2)}, u32[]{:S(2)}) collective-permute-start(f32[28,2048]{1,0:T(8,128)} %edge_lines.1), channel_id=1, source_target_pairs={{64,0}} | collective-permute-start | bytes 688136 | tf_op jit(solution)/shard_map/ppermute | solution.py:703
  20.4 9.3 %copy-start.10 = (f32[28,2048]{1,0:T(8,128)S(1)}, f32[28,2048]{1,0:T(8,128)}, u32[]{:S(2)}) copy-start(f32[28,2048]{1,0:T(8,128)} %edge_lines.1) | copy-start | bytes 688132
  27.3 2.4 %copy-start = (f32[32,336,128]{2,1,0:T(8,128)}, f32[32,336,128]{2,1,0:T(8,128)S(1)}, u32[]{:S(2)}) copy-start(f32[32,336,128]{2,1,0:T(8,128)S(1)} %relayout.1) | copy-start | bytes 16515076
  29.8 12.4 %copy-start.4 = (bf16[256,256]{1,0:T(8,128)(2,1)S(1)}, bf16[256,256]{1,0:T(8,128)(2,1)}, u32[]{:S(2)}) copy-start(bf16[256,256]{1,0:T(8,128)(2,1)} %constant.38.clone.back_table_ref) | copy-start | bytes 393220
  29.8 12.4 %copy-start.5 = (bf16[256,256]{1,0:T(8,128)(2,1)S(1)}, bf16[256,256]{1,0:T(8,128)(2,1)}, u32[]{:S(2)}) copy-start(bf16[256,256]{1,0:T(8,128)(2,1)} %constant.37.clone.table_ref) | copy-start | bytes 393220
  29.8 12.3 %copy-start.6 = (f32[256,128]{1,0:T(8,128)S(1)}, f32[256,128]{1,0:T(8,128)}, u32[]{:S(2)}) copy-start(f32[256,128]{1,0:T(8,128)} %constant.36.clone.back_twiddle_ref) | copy-start | bytes 393220
  29.8 12.3 %copy-start.7 = (f32[256,128]{1,0:T(8,128)S(1)}, f32[256,128]{1,0:T(8,128)}, u32[]{:S(2)}) copy-start(f32[256,128]{1,0:T(8,128)} %constant.35.clone.twiddle_ref) | copy-start | bytes 393220
  51.3 29.8 %copy-start.2 = (bf16[512,256]{1,0:T(8,128)(2,1)S(1)}, bf16[512,256]{1,0:T(8,128)(2,1)}, u32[]{:S(2)}) copy-start(bf16[512,256]{1,0:T(8,128)(2,1)} %constant.39.clone.table_ref) | copy-start | bytes 786436
  51.3 29.8 %copy-start.8 = (f32[16,128]{1,0:T(8,128)S(1)}, f32[16,128]{1,0:T(8,128)}, u32[]{:S(2)}) copy-start(f32[16,128]{1,0:T(8,128)} %constant.40.clone.twiddle_ref) | copy-start | bytes 24580

commit v4 on v3

--- a/solution.py
+++ b/solution.py
@@ -371,13 +371,18 @@
                 row = 2 * k * P1_ALL + place * P1_ALL + OWNED * j
                 save_pair(pl.multiple_of(row, 2 * OWNED), jnp.concatenate(out[j : j + 2], axis=0))
 
-    def forward_dot(k, first, second):
+    group = 5
+
+    def forward_dot(k, count):
         rows = 2 * P1_ALL
         base = k * rows if isinstance(k, int) else pl.multiple_of(k * rows, 2 * OWNED)
-        both = dot(pair_ref[pl.ds(base, rows), :], table_ref[...])
-        whole_line = both[:, :LANES] + both[:, LANES:]
-        spec_ref[pl.ds(first * P1_ALL, P1_ALL), :] = whole_line[:P1_ALL]
-        spec_ref[pl.ds(second * P1_ALL, P1_ALL), :] = whole_line[P1_ALL:]
+        both = dot(pair_ref[pl.ds(base, count * rows), :], table_ref[...])
+        lines = both[:, :LANES] + both[:, LANES:]
+        for i in range(count):
+            first = k + i
+            second = half if count == 1 else ROWS - first
+            spec_ref[pl.ds(first * P1_ALL, P1_ALL), :] = lines[i * rows : i * rows + P1_ALL]
+            spec_ref[pl.ds(second * P1_ALL, P1_ALL), :] = lines[i * rows + P1_ALL : (i + 1) * rows]
 
     twist(0, [0], False)
     cos_edge = blocks(sums_ref, half * P1_ALL, len(kinds))
@@ -385,16 +390,19 @@
     edge = [v * table[kind][0] + pltpu.roll(v, X_ROWS, 1) * table[kind][1] for v, kind in zip(cos_edge, kinds)]
     for j in range(0, len(kinds), 2):
         save_pair(P1_ALL + OWNED * j, jnp.concatenate(edge[j : j + 2], axis=0))
-    forward_dot(0, 0, half)
-    twist(1, [1, ROWS - 1], True)
-
-    def twist_step(k, carry):
-        forward_dot(k - 1, k - 1, ROWS + 1 - k)
+    forward_dot(0, 1)
+    for k in range(1, 1 + group):
         twist(k, [k, ROWS - k], True)
+
+    def twist_step(step, carry):
+        first = 1 + group * step
+        forward_dot(first - group, group)
+        for i in range(group):
+            twist(first + i, [first + i, ROWS - first - i], True)
         return carry
 
-    lax.fori_loop(2, half, twist_step, 0)
-    forward_dot(half - 1, half - 1, half + 1)
+    lax.fori_loop(1, (half - 1) // group, twist_step, 0)
+    forward_dot(half - group, group)
     fetch.wait()
 
     def mix(spectra, coefficient, edge=False):
@@ -463,18 +471,19 @@
         both = dot(pair_ref[pl.ds(p1 * P1_ROWS, rows), :], back_table_ref[...])
         back_ref[pl.ds(p1 * P1_ROWS, rows), :] = both[:, :LANES] + both[:, LANES:]
 
-    mix_line(0)
-    mix_line(1)
+    span = 8
+    for p1 in range(span):
+        mix_line(p1)
 
     def mix_step(step, carry):
-        p1 = pl.multiple_of(2 * step, 2)
-        backward_dot(p1 - 2, 2 * P1_ROWS)
-        mix_line(p1)
-        mix_line(p1 + 1)
+        p1 = pl.multiple_of(span * step, span)
+        backward_dot(p1 - span, span * P1_ROWS)
+        for i in range(span):
+            mix_line(p1 + i)
         return carry
 
-    lax.fori_loop(1, half, mix_step, 0)
-    backward_dot(ROWS - 2, 2 * P1_ROWS)
+    lax.fori_loop(1, ROWS // span, mix_step, 0)
+    backward_dot(ROWS - span, span * P1_ROWS)
 
     count = LAYERS * COMPS
 

time: 83.8 us -> 81.5 us (0.973)
  Pallas kernels: 23.5 us -> 21.1 us
    pallas_call x1, Pallas kernels: 9.11 us -> 6.75 us  [spectral(): pl.pallas_call(spectral_kernel, in_specs=[VMEM, HBM] + [VMEM] * 5, out_sp...]
  transfers between devices with their start and end apart: 2 -> 2, of which waited for: 1 -> 1; matrix products, arithmetic and copies ran while one was open for 1% -> 1% of each run, Pallas kernels for 11% -> 12%
where the time goes in v4:
time: 81.5 us; the launch traced here: 81 us
  blocking collectives  29.7 us (36%)
  Pallas kernels  21.1 us (26%)
  starting transfers between devices  12.2 us (15%)
  waiting for transfers between devices  11.5 us (14%)
  local copies, waits for them, and re-layouts  6.09 us (7%)
    all_to_all x1, blocking collectives, exchange(): lax.all_to_all(lines.reshape(DEVICES, SLOT, LANES), ('layer', 'row'), 0,...  29.7 us
    all_to_all x1, waiting for transfers between devices, exchange(): lax.all_to_all(lines.reshape(DEVICES, SLOT, LANES), ('layer', 'row'), 0,...  11.5 us
    all_to_all x1, starting transfers between devices, exchange(): lax.all_to_all(lines.reshape(DEVICES, SLOT, LANES), ('layer', 'row'), 0,...  11.5 us
    pallas_call x1, Pallas kernels, relayout(): pl.pallas_call(relayout_kernel, grid=(groups,), in_specs=[pl.BlockSpec(me...  6.85 us
    pallas_call x1, Pallas kernels, spectral(): pl.pallas_call(spectral_kernel, in_specs=[VMEM, HBM] + [VMEM] * 5, out_sp...  6.75 us
    unnamed x22, local copies, waits for them, and re-layouts  5.5 us
    pallas_call x1, Pallas kernels, forward_y(): pl.pallas_call(forward_y_kernel, in_specs=[VMEM] * 3, out_specs=HBM, out_...  2.59 us
    pallas_call x1, Pallas kernels, edge_lines(): pl.pallas_call(edge_kernel, in_specs=[HBM], out_specs=VMEM, out_shape=jax...  2.57 us
  transfers between devices with their start and end apart: 2, of which 1 were waited for; matrix products, arithmetic and copies ran while one was open for 1% of the time, Pallas kernels for 12%

profile of v4, /device:TPU:1, one launch (start us, length us, event | category | flops | bytes accessed | tf_op | source)
XLA Modules:
  0.0 81.0 jit_solution(2103499845944719200)
XLA Ops:
  0.0 1.4 %copy-done.1 = f32[3,1,64,2048]{3,2,1,0:T(8,128)S(1)} copy-done((f32[3,1,64,2048]{3,2,1,0:T(8,128)S(1)}, f32[3,1,64,2048]{3,2,1,0:T(8,128)}, u32[]{:S(2)}) %copy-start.1) | copy-done | bytes 1572888
  1.4 0.9 %copy-done.3 = bf16[512,256]{1,0:T(8,128)(2,1)S(1)} copy-done((bf16[512,256]{1,0:T(8,128)(2,1)S(1)}, bf16[512,256]{1,0:T(8,128)(2,1)}, u32[]{:S(2)}) %copy-start.3) | copy-done | bytes 262168
  2.4 0.7 copy-done.9
  3.1 2.6 %forward_y.1 = f32[128,24,128]{2,1,0:T(8,128)} custom-call(f32[192,2048]{1,0:T(8,128)S(1)} %bitcast.17, bf16[512,256]{1,0:T(8,128)(2,1)S(1)} %copy-done.3, f32[16,128]{1,0:T(8,128)S(1)} %copy-done.9), custom_call_target="tpu_custom_call" | custom-call | tf_op jit(solution)/shard_map/forward_y/pallas_call | solution.py:616
  5.7 11.5 %all-to-all-start = ((f32[128,24,128]{2,1,0:T(8,128)}), f32[128,24,128]{2,1,0:T(8,128)S(1)}, u32[]{:S(2)}, u32[]{:S(2)}) async-start(f32[128,24,128]{2,1,0:T(8,128)} %forward_y.1), calls=%async_computation | async-start | bytes 3145728 | tf_op jit(solution)/shard_map/all_to_all | solution.py:702
  17.2 2.6 %edge_lines.1 = f32[28,2048]{1,0:T(8,128)} custom-call(f32[7,6,16,2048]{3,2,1,0:T(8,128)} %kernel_hbm.1), custom_call_target="tpu_custom_call" | custom-call | tf_op jit(solution)/shard_map/edge_lines/pallas_call | solution.py:599
  19.7 0.7 collective-permute-start
  20.4 6.8 %relayout.1 = f32[32,336,128]{2,1,0:T(8,128)S(1)} custom-call(s32[1]{0:T(128)} %bitcast.2.flag_ref, f32[672,2048]{1,0:T(8,128)} %bitcast.18), custom_call_target="tpu_custom_call" | custom-call | tf_op jit(solution)/shard_map/relayout/pallas_call | solution.py:636
  27.3 2.4 %copy-done = f32[32,336,128]{2,1,0:T(8,128)} copy-done((f32[32,336,128]{2,1,0:T(8,128)}, f32[32,336,128]{2,1,0:T(8,128)S(1)}, u32[]{:S(2)}) %copy-start) | copy-done | bytes 5505048
  29.7 0.0 collective-permute-done
  29.7 0.0 copy-done.10
  29.8 0.0 copy-start.4
  29.8 0.0 copy-start.5
  29.8 0.0 copy-start.6
  29.8 0.0 copy-start.7
  29.8 0.3 reshape.38
  30.1 0.3 copy.15
  30.4 0.2 pad_maximum_fusion
  30.6 11.5 %all-to-all-done = f32[128,24,128]{2,1,0:T(8,128)S(1)} async-done(((f32[128,24,128]{2,1,0:T(8,128)}), f32[128,24,128]{2,1,0:T(8,128)S(1)}, u32[]{:S(2)}, u32[]{:S(2)}) %all-to-all-start) | async-done | bytes 1572896 | tf_op jit(solution)/shard_map/all_to_all | solution.py:702
  42.1 6.8 %spectral.1 = f32[3072,128]{1,0:T(8,128)S(1)} custom-call(f32[3072,128]{1,0:T(8,128)S(1)} %bitcast.13, f32[10752,128]{1,0:T(8,128)} %bitcast.12, f32[896,128]{1,0:T(8,128)S(1)} %bitcast.16, f32[256,128]{1,0:T(8,128)S(1)} %copy-done.7, f32[256,128]{1,0:T(8,128)S(1)} %copy-done.6, bf16[256,256]{1,0:T(8,128)(2,1)S(1)} %copy-done.5, bf16[256,256]{1,0:T(8,128)(2,1)S(1)} %copy-done.4), custom_call_target="tpu_custom_call" | custom-call | tf_op jit(solution)/shard_map/spectral/pallas_call | solution.py:654
  48.9 0.0 copy-start.2
  48.9 0.0 copy-start.8
  48.9 29.7 %all_to_all.10 = f32[128,24,128]{2,1,0:T(8,128)S(1)} all-to-all(f32[128,24,128]{2,1,0:T(8,128)S(1)} %bitcast.14), channel_id=1, replica_groups=mesh['layer'=4,'row'=32] {'layer','row'}, dimensions={0} | all-to-all | bytes 3145728 | tf_op jit(solution)/shard_map/all_to_all | solution.py:702
  78.7 2.4 %inverse_y.1 = f32[192,2048]{1,0:T(8,128)} custom-call(f32[3072,128]{1,0:T(8,128)S(1)} %bitcast.15, bf16[512,256]{1,0:T(8,128)(2,1)S(1)} %copy-done.2, f32[16,128]{1,0:T(8,128)S(1)} %copy-done.8), custom_call_target="tpu_custom_call" | custom-call | tf_op jit(solution)/shard_map/inverse_y/pallas_call | solution.py:684
  (12 shorter events, 0.1 us)
Async XLA Ops:
  0.0 1.4 %copy-start.1 = (f32[3,1,64,2048]{3,2,1,0:T(8,128)S(1)}, f32[3,1,64,2048]{3,2,1,0:T(8,128)}, u32[]{:S(2)}) copy-start(f32[3,1,64,2048]{3,2,1,0:T(8,128)} %param.10) | copy-start | bytes 4718596
  1.4 0.9 %copy-start.3 = (bf16[512,256]{1,0:T(8,128)(2,1)S(1)}, bf16[512,256]{1,0:T(8,128)(2,1)}, u32[]{:S(2)}) copy-start(bf16[512,256]{1,0:T(8,128)(2,1)} %constant.33.clone.table_ref) | copy-start | bytes 786436
  2.4 0.7 copy-start.9
  5.7 36.5 %all-to-all-start = ((f32[128,24,128]{2,1,0:T(8,128)}), f32[128,24,128]{2,1,0:T(8,128)S(1)}, u32[]{:S(2)}, u32[]{:S(2)}) async-start(f32[128,24,128]{2,1,0:T(8,128)} %forward_y.1), calls=%async_computation | async-start | bytes 3145728 | tf_op jit(solution)/shard_map/all_to_all | solution.py:702
  19.7 10.0 %collective-permute-start = (f32[28,2048]{1,0:T(8,128)}, f32[28,2048]{1,0:T(8,128)S(1)}, u32[]{:S(2)}, u32[]{:S(2)}) collective-permute-start(f32[28,2048]{1,0:T(8,128)} %edge_lines.1), channel_id=1, source_target_pairs={{64,0}} | collective-permute-start | bytes 688136 | tf_op jit(solution)/shard_map/ppermute | solution.py:712
  20.4 9.3 %copy-start.10 = (f32[28,2048]{1,0:T(8,128)S(1)}, f32[28,2048]{1,0:T(8,128)}, u32[]{:S(2)}) copy-start(f32[28,2048]{1,0:T(8,128)} %edge_lines.1) | copy-start | bytes 688132
  27.3 2.4 %copy-start = (f32[32,336,128]{2,1,0:T(8,128)}, f32[32,336,128]{2,1,0:T(8,128)S(1)}, u32[]{:S(2)}) copy-start(f32[32,336,128]{2,1,0:T(8,128)S(1)} %relayout.1) | copy-start | bytes 16515076
  29.8 12.4 %copy-start.4 = (bf16[256,256]{1,0:T(8,128)(2,1)S(1)}, bf16[256,256]{1,0:T(8,128)(2,1)}, u32[]{:S(2)}) copy-start(bf16[256,256]{1,0:T(8,128)(2,1)} %constant.38.clone.back_table_ref) | copy-start | bytes 393220
  29.8 12.4 %copy-start.5 = (bf16[256,256]{1,0:T(8,128)(2,1)S(1)}, bf16[256,256]{1,0:T(8,128)(2,1)}, u32[]{:S(2)}) copy-start(bf16[256,256]{1,0:T(8,128)(2,1)} %constant.37.clone.table_ref) | copy-start | bytes 393220
  29.8 12.3 %copy-start.6 = (f32[256,128]{1,0:T(8,128)S(1)}, f32[256,128]{1,0:T(8,128)}, u32[]{:S(2)}) copy-start(f32[256,128]{1,0:T(8,128)} %constant.36.clone.back_twiddle_ref) | copy-start | bytes 393220
  29.8 12.3 %copy-start.7 = (f32[256,128]{1,0:T(8,128)S(1)}, f32[256,128]{1,0:T(8,128)}, u32[]{:S(2)}) copy-start(f32[256,128]{1,0:T(8,128)} %constant.35.clone.twiddle_ref) | copy-start | bytes 393220
  48.9 29.8 %copy-start.2 = (bf16[512,256]{1,0:T(8,128)(2,1)S(1)}, bf16[512,256]{1,0:T(8,128)(2,1)}, u32[]{:S(2)}) copy-start(bf16[512,256]{1,0:T(8,128)(2,1)} %constant.39.clone.table_ref) | copy-start | bytes 786436
  48.9 29.8 %copy-start.8 = (f32[16,128]{1,0:T(8,128)S(1)}, f32[16,128]{1,0:T(8,128)}, u32[]{:S(2)}) copy-start(f32[16,128]{1,0:T(8,128)} %constant.40.clone.twiddle_ref) | copy-start | bytes 24580

commit v5 on v4

--- a/solution.py
+++ b/solution.py
@@ -191,22 +191,23 @@
         lanes = pl.ds(LANES * j, LANES)
         for i, (source, target) in enumerate([((0, 3), (0, 3)), ((4, 1), (3, 1))]):
             copy = pltpu.make_async_copy(
-                kernel_hbm.at[:, pl.ds(*source), pl.ds(0, OWNED), lanes],
+                kernel_hbm.at[:, pl.ds(*source), pl.ds(0, 1), lanes],
                 tiles_ref.at[j, :, pl.ds(*target)],
                 sem.at[j, i],
             )
             copy.start()
             copies.append(copy)
-    flat = tiles_ref.reshape(n_tiles * EDGES * OWNED, LANES)
+    flat = tiles_ref.reshape(n_tiles * EDGES, LANES)
     for j in range(n_tiles):
         copies[2 * j].wait()
         copies[2 * j + 1].wait()
-        out_ref[:, LANES * j : LANES * (j + 1)] = flat[pl.ds(j * EDGES * OWNED, EDGES, stride=OWNED), :]
+        out_ref[:, LANES * j : LANES * (j + 1)] = flat[pl.ds(j * EDGES, EDGES), :]
 
 
 def forward_y_kernel(x_ref, table_ref, twiddle_ref, out_hbm, high_ref, low_ref, out_ref, sem):
     slots = out_ref.reshape(DEVICES, SLOT, LANES)
     saves = []
+    edges = []
     half = DEVICES // 2
     middle = COARSE // 2
     group = 16
@@ -237,18 +238,20 @@
                     high_ref[rows, LANES:], low_ref[rows, LANES:] = zero, zero
                 else:
                     high_ref[rows, LANES:], low_ref[rows, LANES:] = split_pair(imag)
-        size = (middle + 1) * X_ROWS
-        out = triple_dot(high_ref[base : base + size, :], low_ref[base : base + size, :], table_ref)
+        edges.append(jnp.concatenate(nyquist, axis=0))
+    out = triple_dot(high_ref[...], low_ref[...], table_ref)
+    for comp in range(COMPS):
 
         def pick(k):
-            rows = out[k * X_ROWS : (k + 1) * X_ROWS]
+            row = (comp * (middle + 1) + k) * X_ROWS
+            rows = out[row : row + X_ROWS]
             return rows[:, :LANES], rows[:, LANES:]
 
         for k in range(middle):
             real, imag = pick(k)
             if k == 0:
                 last_real, last_imag = pick(middle)
-                imag = jnp.where(lane == 0, jnp.concatenate(nyquist, axis=0), imag)
+                imag = jnp.where(lane == 0, edges[comp], imag)
                 real = jnp.where(lane < half, real, last_real)
                 imag = jnp.where(lane < half, imag, last_imag)
             block = jnp.concatenate([real, imag], axis=0).T
@@ -535,6 +538,7 @@
     lane = lax.broadcasted_iota(jnp.int32, (X_ROWS, LANES), 1)
     alternate = 1.0 - 2.0 * (lax.broadcasted_iota(jnp.int32, (group, FINE), 1) % 2).astype(F32)
     copies = []
+    columns = []
     for comp in range(COMPS):
         size = (middle + 1) * X_ROWS
         base = comp * size
@@ -556,9 +560,11 @@
                 scale = jnp.where(lane < half, jnp.where(lane == 0, 0.5, 1.0), 0.0)
                 real, imag = real * scale, imag * scale
             put(k, real, imag)
-        lines_ref[base : base + size, :] = triple_dot(
-            high_ref[base : base + size, :], low_ref[base : base + size, :], table_ref
-        )
+        columns.append(nyquist)
+    lines_ref[...] = triple_dot(high_ref[...], low_ref[...], table_ref)
+    for comp in range(COMPS):
+        base = comp * (middle + 1) * X_ROWS
+        nyquist = columns[comp]
         for g in range(X_ROWS // group):
             cos_in = [None] * (middle + 1)
             sin_in = [None] * (middle + 1)
@@ -602,7 +608,7 @@
         out_specs=VMEM,
         out_shape=jax.ShapeDtypeStruct((EDGES, CELLS), F32),
         scratch_shapes=[
-            pltpu.VMEM((CELLS // LANES, OFFSETS, EDGE_PARTS, OWNED, LANES), F32),
+            pltpu.VMEM((CELLS // LANES, OFFSETS, EDGE_PARTS, 1, LANES), F32),
             pltpu.SemaphoreType.DMA((CELLS // LANES, 2)),
         ],
         compiler_params=params(58),

time: 81.5 us -> 80.7 us (level)
  Pallas kernels: 21.1 us -> 19.9 us
  transfers between devices with their start and end apart: 2 -> 2, of which waited for: 1 -> 1; matrix products, arithmetic and copies ran while one was open for 1% -> 1% of each run, Pallas kernels for 12% -> 11%
where the time goes in v5:
time: 80.7 us; the launch traced here: 80.2 us
  blocking collectives  29.6 us (37%)
  Pallas kernels  19.9 us (25%)
  starting transfers between devices  12.2 us (15%)
  waiting for transfers between devices  12.1 us (15%)
  local copies, waits for them, and re-layouts  6.09 us (8%)
    all_to_all x1, blocking collectives, exchange(): lax.all_to_all(lines.reshape(DEVICES, SLOT, LANES), ('layer', 'row'), 0,...  29.6 us
    all_to_all x1, waiting for transfers between devices, exchange(): lax.all_to_all(lines.reshape(DEVICES, SLOT, LANES), ('layer', 'row'), 0,...  12.1 us
    all_to_all x1, starting transfers between devices, exchange(): lax.all_to_all(lines.reshape(DEVICES, SLOT, LANES), ('layer', 'row'), 0,...  11.5 us
    pallas_call x1, Pallas kernels, relayout(): pl.pallas_call(relayout_kernel, grid=(groups,), in_specs=[pl.BlockSpec(me...  6.85 us
    pallas_call x1, Pallas kernels, spectral(): pl.pallas_call(spectral_kernel, in_specs=[VMEM, HBM] + [VMEM] * 5, out_sp...  6.75 us
    unnamed x22, local copies, waits for them, and re-layouts  5.5 us
    pallas_call x1, Pallas kernels, forward_y(): pl.pallas_call(forward_y_kernel, in_specs=[VMEM] * 3, out_specs=HBM, out_...  2.33 us
    pallas_call x1, Pallas kernels, inverse_y(): pl.pallas_call(inverse_y_kernel, in_specs=[VMEM] * 3, out_specs=HBM, out_...  1.98 us
  transfers between devices with their start and end apart: 2, of which 1 were waited for; matrix products, arithmetic and copies ran while one was open for 1% of the time, Pallas kernels for 11%

profile of v5, /device:TPU:1, one launch (start us, length us, event | category | flops | bytes accessed | tf_op | source)
XLA Modules:
  0.0 80.2 jit_solution(7094285918069983363)
XLA Ops:
  0.0 1.4 %copy-done.1 = f32[3,1,64,2048]{3,2,1,0:T(8,128)S(1)} copy-done((f32[3,1,64,2048]{3,2,1,0:T(8,128)S(1)}, f32[3,1,64,2048]{3,2,1,0:T(8,128)}, u32[]{:S(2)}) %copy-start.1) | copy-done | bytes 1572888
  1.4 0.9 %copy-done.3 = bf16[512,256]{1,0:T(8,128)(2,1)S(1)} copy-done((bf16[512,256]{1,0:T(8,128)(2,1)S(1)}, bf16[512,256]{1,0:T(8,128)(2,1)}, u32[]{:S(2)}) %copy-start.3) | copy-done | bytes 262168
  2.4 0.7 copy-done.9
  3.1 2.3 %forward_y.1 = f32[128,24,128]{2,1,0:T(8,128)} custom-call(f32[192,2048]{1,0:T(8,128)S(1)} %bitcast.17, bf16[512,256]{1,0:T(8,128)(2,1)S(1)} %copy-done.3, f32[16,128]{1,0:T(8,128)S(1)} %copy-done.9), custom_call_target="tpu_custom_call" | custom-call | tf_op jit(solution)/shard_map/forward_y/pallas_call | solution.py:622
  5.4 11.5 %all-to-all-start = ((f32[128,24,128]{2,1,0:T(8,128)}), f32[128,24,128]{2,1,0:T(8,128)S(1)}, u32[]{:S(2)}, u32[]{:S(2)}) async-start(f32[128,24,128]{2,1,0:T(8,128)} %forward_y.1), calls=%async_computation | async-start | bytes 3145728 | tf_op jit(solution)/shard_map/all_to_all | solution.py:708
  16.9 2.0 %edge_lines.1 = f32[28,2048]{1,0:T(8,128)} custom-call(f32[7,6,16,2048]{3,2,1,0:T(8,128)} %kernel_hbm.1), custom_call_target="tpu_custom_call" | custom-call | tf_op jit(solution)/shard_map/edge_lines/pallas_call | solution.py:605
  18.9 0.7 collective-permute-start
  19.6 6.8 %relayout.1 = f32[32,336,128]{2,1,0:T(8,128)S(1)} custom-call(s32[1]{0:T(128)} %bitcast.2.flag_ref, f32[672,2048]{1,0:T(8,128)} %bitcast.18), custom_call_target="tpu_custom_call" | custom-call | tf_op jit(solution)/shard_map/relayout/pallas_call | solution.py:642
  26.4 0.0 copy-start
  26.4 2.4 %copy-done = f32[32,336,128]{2,1,0:T(8,128)} copy-done((f32[32,336,128]{2,1,0:T(8,128)}, f32[32,336,128]{2,1,0:T(8,128)S(1)}, u32[]{:S(2)}) %copy-start) | copy-done | bytes 5505048
  28.8 0.0 collective-permute-done
  28.9 0.0 copy-start.4
  28.9 0.0 copy-start.5
  28.9 0.0 copy-start.6
  28.9 0.0 copy-start.7
  28.9 0.3 reshape.38
  29.2 0.3 copy.15
  29.5 0.2 pad_maximum_fusion
  29.7 12.1 %all-to-all-done = f32[128,24,128]{2,1,0:T(8,128)S(1)} async-done(((f32[128,24,128]{2,1,0:T(8,128)}), f32[128,24,128]{2,1,0:T(8,128)S(1)}, u32[]{:S(2)}, u32[]{:S(2)}) %all-to-all-start) | async-done | bytes 1572896 | tf_op jit(solution)/shard_map/all_to_all | solution.py:708
  41.9 6.8 %spectral.1 = f32[3072,128]{1,0:T(8,128)S(1)} custom-call(f32[3072,128]{1,0:T(8,128)S(1)} %bitcast.13, f32[10752,128]{1,0:T(8,128)} %bitcast.12, f32[896,128]{1,0:T(8,128)S(1)} %bitcast.16, f32[256,128]{1,0:T(8,128)S(1)} %copy-done.7, f32[256,128]{1,0:T(8,128)S(1)} %copy-done.6, bf16[256,256]{1,0:T(8,128)(2,1)S(1)} %copy-done.5, bf16[256,256]{1,0:T(8,128)(2,1)S(1)} %copy-done.4), custom_call_target="tpu_custom_call" | custom-call | tf_op jit(solution)/shard_map/spectral/pallas_call | solution.py:660
  48.6 0.0 copy-start.2
  48.7 0.0 copy-start.8
  48.7 29.6 %all_to_all.10 = f32[128,24,128]{2,1,0:T(8,128)S(1)} all-to-all(f32[128,24,128]{2,1,0:T(8,128)S(1)} %bitcast.14), channel_id=1, replica_groups=mesh['layer'=4,'row'=32] {'layer','row'}, dimensions={0} | all-to-all | bytes 3145728 | tf_op jit(solution)/shard_map/all_to_all | solution.py:708
  78.3 2.0 %inverse_y.1 = f32[192,2048]{1,0:T(8,128)} custom-call(f32[3072,128]{1,0:T(8,128)S(1)} %bitcast.15, bf16[512,256]{1,0:T(8,128)(2,1)S(1)} %copy-done.2, f32[16,128]{1,0:T(8,128)S(1)} %copy-done.8), custom_call_target="tpu_custom_call" | custom-call | tf_op jit(solution)/shard_map/inverse_y/pallas_call | solution.py:690
  (12 shorter events, 0.1 us)
Async XLA Ops:
  0.0 1.4 %copy-start.1 = (f32[3,1,64,2048]{3,2,1,0:T(8,128)S(1)}, f32[3,1,64,2048]{3,2,1,0:T(8,128)}, u32[]{:S(2)}) copy-start(f32[3,1,64,2048]{3,2,1,0:T(8,128)} %param.10) | copy-start | bytes 4718596
  1.4 0.9 %copy-start.3 = (bf16[512,256]{1,0:T(8,128)(2,1)S(1)}, bf16[512,256]{1,0:T(8,128)(2,1)}, u32[]{:S(2)}) copy-start(bf16[512,256]{1,0:T(8,128)(2,1)} %constant.33.clone.table_ref) | copy-start | bytes 786436
  2.4 0.7 copy-start.9
  5.4 36.5 %all-to-all-start = ((f32[128,24,128]{2,1,0:T(8,128)}), f32[128,24,128]{2,1,0:T(8,128)S(1)}, u32[]{:S(2)}, u32[]{:S(2)}) async-start(f32[128,24,128]{2,1,0:T(8,128)} %forward_y.1), calls=%async_computation | async-start | bytes 3145728 | tf_op jit(solution)/shard_map/all_to_all | solution.py:708
  18.9 10.0 %collective-permute-start = (f32[28,2048]{1,0:T(8,128)}, f32[28,2048]{1,0:T(8,128)S(1)}, u32[]{:S(2)}, u32[]{:S(2)}) collective-permute-start(f32[28,2048]{1,0:T(8,128)} %edge_lines.1), channel_id=1, source_target_pairs={{64,0}} | collective-permute-start | bytes 688136 | tf_op jit(solution)/shard_map/ppermute | solution.py:718
  19.6 9.3 %copy-start.10 = (f32[28,2048]{1,0:T(8,128)S(1)}, f32[28,2048]{1,0:T(8,128)}, u32[]{:S(2)}) copy-start(f32[28,2048]{1,0:T(8,128)} %edge_lines.1) | copy-start | bytes 688132
  26.4 2.4 %copy-start = (f32[32,336,128]{2,1,0:T(8,128)}, f32[32,336,128]{2,1,0:T(8,128)S(1)}, u32[]{:S(2)}) copy-start(f32[32,336,128]{2,1,0:T(8,128)S(1)} %relayout.1) | copy-start | bytes 16515076
  28.9 13.0 %copy-start.4 = (bf16[256,256]{1,0:T(8,128)(2,1)S(1)}, bf16[256,256]{1,0:T(8,128)(2,1)}, u32[]{:S(2)}) copy-start(bf16[256,256]{1,0:T(8,128)(2,1)} %constant.38.clone.back_table_ref) | copy-start | bytes 393220
  28.9 13.0 %copy-start.5 = (bf16[256,256]{1,0:T(8,128)(2,1)S(1)}, bf16[256,256]{1,0:T(8,128)(2,1)}, u32[]{:S(2)}) copy-start(bf16[256,256]{1,0:T(8,128)(2,1)} %constant.37.clone.table_ref) | copy-start | bytes 393220
  28.9 13.0 %copy-start.6 = (f32[256,128]{1,0:T(8,128)S(1)}, f32[256,128]{1,0:T(8,128)}, u32[]{:S(2)}) copy-start(f32[256,128]{1,0:T(8,128)} %constant.36.clone.back_twiddle_ref) | copy-start | bytes 393220
  28.9 13.0 %copy-start.7 = (f32[256,128]{1,0:T(8,128)S(1)}, f32[256,128]{1,0:T(8,128)}, u32[]{:S(2)}) copy-start(f32[256,128]{1,0:T(8,128)} %constant.35.clone.twiddle_ref) | copy-start | bytes 393220
  48.6 29.6 %copy-start.2 = (bf16[512,256]{1,0:T(8,128)(2,1)S(1)}, bf16[512,256]{1,0:T(8,128)(2,1)}, u32[]{:S(2)}) copy-start(bf16[512,256]{1,0:T(8,128)(2,1)} %constant.39.clone.table_ref) | copy-start | bytes 786436
  48.7 29.6 %copy-start.8 = (f32[16,128]{1,0:T(8,128)S(1)}, f32[16,128]{1,0:T(8,128)}, u32[]{:S(2)}) copy-start(f32[16,128]{1,0:T(8,128)} %constant.40.clone.twiddle_ref) | copy-start | bytes 24580

commit v6 on v5

--- a/solution.py
+++ b/solution.py
@@ -55,34 +55,35 @@
     return table.reshape(COARSE, FINE).astype(np.float32)
 
 
-def lane_pair(coefficient):
-    real = np.concatenate([coefficient.real, coefficient.real], axis=-1)
-    imag = np.concatenate([-coefficient.imag, coefficient.imag], axis=-1)
-    return real, imag
-
-
-def x_twiddle(sign, scale):
-    p1 = np.arange(ROWS)[:, None]
+def x_twiddle(sign, scale, inner):
+    k = np.arange(ROWS // 2 + 1)[:, None]
     t = np.arange(X_ROWS)[None, :]
-    base = scale * np.exp(sign * 2.0j * np.pi * (p1 * t) / CELLS)
-    side = np.where(p1 <= ROWS // 2, 1.0, -1.0) * (sign * 1.0j)
-    kinds = []
-    for kind in (1.0, 1.0j):
-        first = lane_pair(kind * base)
-        second = lane_pair(kind * base * side)
-        kinds.append(np.stack(first + second, axis=1))
-    return np.stack(kinds).astype(np.float32).reshape(2 * ROWS * 4, LANES)
-
-
-def x_table(sign):
+    angle = 2.0 * np.pi * k * t / CELLS
+    cosine = scale * np.cos(angle)
+    sine = scale * sign * np.sin(angle)
+    lines = [
+        np.concatenate([cosine, cosine], axis=1),
+        np.concatenate([sine, sine], axis=1),
+        np.concatenate([inner * sine, -inner * sine], axis=1),
+        np.concatenate([inner * cosine, -inner * cosine], axis=1),
+    ]
+    return np.stack(lines, axis=1).astype(np.float32).reshape(-1, LANES)
+
+
+def x_table(sign, shift):
     index = np.arange(X_ROWS)
-    angle = 2.0 * np.pi * (np.outer(index, index) % X_ROWS) / X_ROWS
+    place = np.outer(index, index + shift) if sign < 0 else np.outer(index + shift, index)
+    angle = 2.0 * np.pi * (place % X_ROWS) / X_ROWS
     real = np.cos(angle)
     imag = sign * np.sin(angle)
     whole = np.block([[real, imag], [-imag, real]])
     high, low = halves(whole)
     line = np.concatenate([high, low], axis=1)
     return np.concatenate([line, line], axis=0)
+
+
+def x_tables(sign):
+    return np.concatenate([x_table(sign, 0), x_table(sign, 1)], axis=0)
 
 
 def real_dft(values):
@@ -254,6 +255,8 @@
                 imag = jnp.where(lane == 0, edges[comp], imag)
                 real = jnp.where(lane < half, real, last_real)
                 imag = jnp.where(lane < half, imag, last_imag)
+            if comp == COMPS - 1:
+                real, imag = -imag, real
             block = jnp.concatenate([real, imag], axis=0).T
             near, far = slot_rows(comp, k)
             if k == 0:
@@ -317,7 +320,7 @@
     for layer in range(LAYERS):
         for comp in range(COMPS):
             line = x_ref[pl.ds(layer * ROWS * SLOT + comp * OWNED, ROWS, stride=SLOT), :]
-            extra_ref[pl.ds(comp * LAYERS + layer, ROWS, stride=EXTRA), :] = jnp.where(lane < X_ROWS, 0.0, line)
+            extra_ref[pl.ds(comp * LAYERS + layer, ROWS, stride=EXTRA), :] = jnp.where((lane < X_ROWS) == (comp == COMPS - 1), line, 0.0)
     fix_ref[...] = jnp.zeros_like(fix_ref)
 
     def store_sums(values, place):
@@ -341,71 +344,60 @@
         values = [extra_ref[r * EXTRA + group * 8 : r * EXTRA + group * 8 + 8, :] for r in range(ROWS)]
         store_sums(values, P1_ROWS + group * 8)
 
-    def factors(ref, p1, kind):
-        base = kind * (ROWS * 4) + p1 * 4
-        return [ref[pl.ds(base + j, 1), :] for j in range(4)]
+    def factors(ref, k):
+        return [ref[pl.ds(4 * k + j, 1), :] for j in range(4)]
 
     def save_pair(row, value):
         high, low = split_pair(value)
         pair_ref[pl.ds(row, value.shape[0]), :LANES] = high
         pair_ref[pl.ds(row, value.shape[0]), LANES:] = low
 
-    kinds = [1 if j % COMPS == 2 else 0 for j in range(LAYERS * COMPS)] + [0, 1]
+    n_blocks = P1_ALL // OWNED
 
     def blocks(ref, row, count):
         return [ref[pl.ds(row + OWNED * j, OWNED), :] for j in range(count)]
 
-    def twist(k, p1_list, with_sin):
-        cos_rows = blocks(sums_ref, pl.multiple_of(k * P1_ALL, OWNED), len(kinds))
-        cos_swap = [pltpu.roll(v, X_ROWS, 1) for v in cos_rows]
-        if with_sin:
-            sin_rows = blocks(sums_ref, pl.multiple_of((half + k) * P1_ALL, OWNED), len(kinds))
-            sin_swap = [pltpu.roll(v, X_ROWS, 1) for v in sin_rows]
-        for place, p1 in enumerate(p1_list):
-            table = [factors(twiddle_ref, p1, kind) for kind in range(2)]
-            out = []
-            for j, kind in enumerate(kinds):
-                f = table[kind]
-                value = cos_rows[j] * f[0] + cos_swap[j] * f[1]
-                if with_sin:
-                    value = value + (sin_rows[j] * f[2] + sin_swap[j] * f[3])
-                out.append(value)
-            for j in range(0, len(kinds), 2):
-                row = 2 * k * P1_ALL + place * P1_ALL + OWNED * j
-                save_pair(pl.multiple_of(row, 2 * OWNED), jnp.concatenate(out[j : j + 2], axis=0))
-
-    group = 5
-
-    def forward_dot(k, count):
-        rows = 2 * P1_ALL
-        base = k * rows if isinstance(k, int) else pl.multiple_of(k * rows, 2 * OWNED)
-        both = dot(pair_ref[pl.ds(base, count * rows), :], table_ref[...])
-        lines = both[:, :LANES] + both[:, LANES:]
-        for i in range(count):
-            first = k + i
-            second = half if count == 1 else ROWS - first
-            spec_ref[pl.ds(first * P1_ALL, P1_ALL), :] = lines[i * rows : i * rows + P1_ALL]
-            spec_ref[pl.ds(second * P1_ALL, P1_ALL), :] = lines[i * rows + P1_ALL : (i + 1) * rows]
-
-    twist(0, [0], False)
-    cos_edge = blocks(sums_ref, half * P1_ALL, len(kinds))
-    table = [factors(twiddle_ref, half, kind) for kind in range(2)]
-    edge = [v * table[kind][0] + pltpu.roll(v, X_ROWS, 1) * table[kind][1] for v, kind in zip(cos_edge, kinds)]
-    for j in range(0, len(kinds), 2):
-        save_pair(P1_ALL + OWNED * j, jnp.concatenate(edge[j : j + 2], axis=0))
-    forward_dot(0, 1)
-    for k in range(1, 1 + group):
-        twist(k, [k, ROWS - k], True)
-
-    def twist_step(step, carry):
-        first = 1 + group * step
-        forward_dot(first - group, group)
-        for i in range(group):
-            twist(first + i, [first + i, ROWS - first - i], True)
-        return carry
-
-    lax.fori_loop(1, (half - 1) // group, twist_step, 0)
-    forward_dot(half - group, group)
+    def save_line(p1, values):
+        for j in range(0, n_blocks, 2):
+            save_pair(p1 * P1_ALL + OWNED * j, jnp.concatenate(values[j : j + 2], axis=0))
+
+    def twist(k):
+        f = factors(twiddle_ref, k)
+        cos_rows = blocks(sums_ref, k * P1_ALL, n_blocks)
+        if k in (0, half):
+            even = [c * f[0] for c in cos_rows]
+            odd = [c * f[2] for c in cos_rows]
+        else:
+            sin_rows = blocks(sums_ref, (half + k) * P1_ALL, n_blocks)
+            even = [c * f[0] + v * f[1] for c, v in zip(cos_rows, sin_rows)]
+            odd = [c * f[2] - v * f[3] for c, v in zip(cos_rows, sin_rows)]
+        if k == 0:
+            save_line(0, even)
+            return
+        odd = [pltpu.roll(v, X_ROWS, 1) for v in odd]
+        if k != half:
+            save_line(k, [a + b for a, b in zip(even, odd)])
+        save_line(ROWS - k, [a - b for a, b in zip(even, odd)])
+
+    size = 2 * LANES
+
+    def forward_dot(first, count, which):
+        rows = pl.ds(first * P1_ALL, count * P1_ALL)
+        both = dot(pair_ref[rows, :], table_ref[which * size : (which + 1) * size, :])
+        spec_ref[rows, :] = both[:, :LANES] + both[:, LANES:]
+
+    for k in range(6):
+        twist(k)
+    forward_dot(0, 6, 0)
+    forward_dot(27, 5, 1)
+    for k in range(6, 11):
+        twist(k)
+    forward_dot(6, 5, 0)
+    forward_dot(22, 5, 1)
+    for k in range(11, half + 1):
+        twist(k)
+    forward_dot(11, 5, 0)
+    forward_dot(half, 6, 1)
     fetch.wait()
 
     def mix(spectra, coefficient, edge=False):
@@ -471,7 +463,9 @@
             save_pair(row + OWNED * j, jnp.concatenate(flat[j : j + 2], axis=0))
 
     def backward_dot(p1, rows):
-        both = dot(pair_ref[pl.ds(p1 * P1_ROWS, rows), :], back_table_ref[...])
+        which = p1 // half
+        base = which * size if isinstance(p1, int) else pl.multiple_of(which * size, size)
+        both = dot(pair_ref[pl.ds(p1 * P1_ROWS, rows), :], back_table_ref[pl.ds(base, size), :])
         back_ref[pl.ds(p1 * P1_ROWS, rows), :] = both[:, :LANES] + both[:, LANES:]
 
     span = 8
@@ -489,29 +483,25 @@
     backward_dot(ROWS - span, span * P1_ROWS)
 
     count = LAYERS * COMPS
-
-    def untwist_edge(p1, slot):
-        table = [factors(back_twiddle_ref, p1, kind) for kind in range(2)]
-        for j, value in enumerate(blocks(back_ref, p1 * P1_ROWS, count)):
-            f = table[kinds[j]]
-            sums_ref[pl.ds(slot * P1_ROWS + OWNED * j, OWNED), :] = value * f[0] + pltpu.roll(value, X_ROWS, 1) * f[1]
-
-    untwist_edge(0, 0)
-    untwist_edge(half, half)
+    f = factors(back_twiddle_ref, 0)
+    for j, value in enumerate(blocks(back_ref, 0, count)):
+        sums_ref[pl.ds(OWNED * j, OWNED), :] = value * f[0]
+    f = factors(back_twiddle_ref, half)
+    for j, value in enumerate(blocks(back_ref, half * P1_ROWS, count)):
+        swap = pltpu.roll(value, X_ROWS, 1)
+        sums_ref[pl.ds(half * P1_ROWS + OWNED * j, OWNED), :] = value * f[0] - swap * f[2]
 
     def untwist_step(k, carry):
-        near = [factors(back_twiddle_ref, k, kind) for kind in range(2)]
-        far = [factors(back_twiddle_ref, ROWS - k, kind) for kind in range(2)]
-        near_rows = blocks(back_ref, pl.multiple_of(k * P1_ROWS, OWNED), count)
-        far_rows = blocks(back_ref, pl.multiple_of((ROWS - k) * P1_ROWS, OWNED), count)
+        f = factors(back_twiddle_ref, k)
+        near = blocks(back_ref, pl.multiple_of(k * P1_ROWS, OWNED), count)
+        far = blocks(back_ref, pl.multiple_of((ROWS - k) * P1_ROWS, OWNED), count)
         cos_base = pl.multiple_of(k * P1_ROWS, OWNED)
         sin_base = pl.multiple_of((half + k) * P1_ROWS, OWNED)
         for j in range(count):
-            n, f = near[kinds[j]], far[kinds[j]]
-            a, b = near_rows[j], far_rows[j]
-            a_swap, b_swap = pltpu.roll(a, X_ROWS, 1), pltpu.roll(b, X_ROWS, 1)
-            sums_ref[pl.ds(cos_base + OWNED * j, OWNED), :] = (a * n[0] + a_swap * n[1]) + (b * f[0] + b_swap * f[1])
-            sums_ref[pl.ds(sin_base + OWNED * j, OWNED), :] = (a * n[2] + a_swap * n[3]) + (b * f[2] + b_swap * f[3])
+            plus = near[j] + far[j]
+            swap = pltpu.roll(near[j] - far[j], X_ROWS, 1)
+            sums_ref[pl.ds(cos_base + OWNED * j, OWNED), :] = plus * f[0] + swap * f[2]
+            sums_ref[pl.ds(sin_base + OWNED * j, OWNED), :] = swap * f[3] - plus * f[1]
         return carry
 
     lax.fori_loop(1, half, untwist_step, 0)
@@ -554,6 +544,8 @@
                 far = slot_rows(comp, middle)[1]
             block = jnp.concatenate([x_ref[near, :], x_ref[far, :]], axis=0).T
             real, imag = block[:X_ROWS], block[X_ROWS:]
+            if comp == COMPS - 1:
+                real, imag = -imag, real
             if k == 0:
                 nyquist = imag[:, :1]
                 put(middle, jnp.where(lane < half, 0.0, real), jnp.where(lane < half, 0.0, imag))
@@ -655,8 +647,8 @@
 
 
 def spectral(lines, kernel, delta):
-    twiddle = x_twiddle(-1.0, 1.0)
-    back_twiddle = x_twiddle(1.0, -1.0 / (CELLS * CELLS))
+    twiddle = x_twiddle(-1.0, 1.0, 1.0)
+    back_twiddle = x_twiddle(1.0, -1.0 / (CELLS * CELLS), -1.0)
     return pl.pallas_call(
         spectral_kernel,
         in_specs=[VMEM, HBM] + [VMEM] * 5,
@@ -680,8 +672,8 @@
         delta,
         jnp.asarray(twiddle),
         jnp.asarray(back_twiddle),
-        jnp.asarray(x_table(-1.0)),
-        jnp.asarray(x_table(1.0)),
+        jnp.asarray(x_tables(-1.0)),
+        jnp.asarray(x_tables(1.0)),
     )
 
 

time: 80.7 us -> 80.4 us (level)
  no operation moved by 1% of the time
where the time goes in v6:
time: 80.4 us; the launch traced here: 80 us
  blocking collectives  29.5 us (37%)
  Pallas kernels  19.6 us (24%)
  starting transfers between devices  12.2 us (15%)
  waiting for transfers between devices  12.1 us (15%)
  local copies, waits for them, and re-layouts  6.09 us (8%)
    all_to_all x1, blocking collectives, exchange(): lax.all_to_all(lines.reshape(DEVICES, SLOT, LANES), ('layer', 'row'), 0,...  29.5 us
    all_to_all x1, waiting for transfers between devices, exchange(): lax.all_to_all(lines.reshape(DEVICES, SLOT, LANES), ('layer', 'row'), 0,...  12.1 us
    all_to_all x1, starting transfers between devices, exchange(): lax.all_to_all(lines.reshape(DEVICES, SLOT, LANES), ('layer', 'row'), 0,...  11.5 us
    pallas_call x1, Pallas kernels, relayout(): pl.pallas_call(relayout_kernel, grid=(groups,), in_specs=[pl.BlockSpec(me...  6.85 us
    pallas_call x1, Pallas kernels, spectral(): pl.pallas_call(spectral_kernel, in_specs=[VMEM, HBM] + [VMEM] * 5, out_sp...  6.53 us
    unnamed x22, local copies, waits for them, and re-layouts  5.5 us
    pallas_call x1, Pallas kernels, forward_y(): pl.pallas_call(forward_y_kernel, in_specs=[VMEM] * 3, out_specs=HBM, out_...  2.33 us
    pallas_call x1, Pallas kernels, inverse_y(): pl.pallas_call(inverse_y_kernel, in_specs=[VMEM] * 3, out_specs=HBM, out_...  1.98 us
  transfers between devices with their start and end apart: 2, of which 1 were waited for; matrix products, arithmetic and copies ran while one was open for 1% of the time, Pallas kernels for 11%

profile of v6, /device:TPU:1, one launch (start us, length us, event | category | flops | bytes accessed | tf_op | source)
XLA Modules:
  0.0 80.0 jit_solution(675102184663198748)
XLA Ops:
  0.0 1.4 %copy-done.1 = f32[3,1,64,2048]{3,2,1,0:T(8,128)S(1)} copy-done((f32[3,1,64,2048]{3,2,1,0:T(8,128)S(1)}, f32[3,1,64,2048]{3,2,1,0:T(8,128)}, u32[]{:S(2)}) %copy-start.1) | copy-done | bytes 1572888
  1.4 0.9 %copy-done.5 = bf16[512,256]{1,0:T(8,128)(2,1)S(1)} copy-done((bf16[512,256]{1,0:T(8,128)(2,1)S(1)}, bf16[512,256]{1,0:T(8,128)(2,1)}, u32[]{:S(2)}) %copy-start.5) | copy-done | bytes 262168
  2.4 0.7 copy-done.9
  3.1 2.3 %forward_y.1 = f32[128,24,128]{2,1,0:T(8,128)} custom-call(f32[192,2048]{1,0:T(8,128)S(1)} %bitcast.17, bf16[512,256]{1,0:T(8,128)(2,1)S(1)} %copy-done.5, f32[16,128]{1,0:T(8,128)S(1)} %copy-done.9), custom_call_target="tpu_custom_call" | custom-call | tf_op jit(solution)/shard_map/forward_y/pallas_call | solution.py:614
  5.4 11.5 %all-to-all-start = ((f32[128,24,128]{2,1,0:T(8,128)}), f32[128,24,128]{2,1,0:T(8,128)S(1)}, u32[]{:S(2)}, u32[]{:S(2)}) async-start(f32[128,24,128]{2,1,0:T(8,128)} %forward_y.1), calls=%async_computation | async-start | bytes 3145728 | tf_op jit(solution)/shard_map/all_to_all | solution.py:700
  16.9 2.0 %edge_lines.1 = f32[28,2048]{1,0:T(8,128)} custom-call(f32[7,6,16,2048]{3,2,1,0:T(8,128)} %kernel_hbm.1), custom_call_target="tpu_custom_call" | custom-call | tf_op jit(solution)/shard_map/edge_lines/pallas_call | solution.py:597
  18.9 0.7 collective-permute-start
  19.6 6.8 %relayout.1 = f32[32,336,128]{2,1,0:T(8,128)S(1)} custom-call(s32[1]{0:T(128)} %bitcast.2.flag_ref, f32[672,2048]{1,0:T(8,128)} %bitcast.18), custom_call_target="tpu_custom_call" | custom-call | tf_op jit(solution)/shard_map/relayout/pallas_call | solution.py:634
  26.4 2.4 %copy-done = f32[32,336,128]{2,1,0:T(8,128)} copy-done((f32[32,336,128]{2,1,0:T(8,128)}, f32[32,336,128]{2,1,0:T(8,128)S(1)}, u32[]{:S(2)}) %copy-start) | copy-done | bytes 5505048
  28.8 0.0 collective-permute-done
  28.9 0.0 copy-start.2
  28.9 0.0 copy-start.3
  28.9 0.0 copy-start.6
  28.9 0.0 copy-start.7
  28.9 0.3 reshape.38
  29.2 0.3 copy.15
  29.5 0.2 pad_maximum_fusion
  29.7 12.1 %all-to-all-done = f32[128,24,128]{2,1,0:T(8,128)S(1)} async-done(((f32[128,24,128]{2,1,0:T(8,128)}), f32[128,24,128]{2,1,0:T(8,128)S(1)}, u32[]{:S(2)}, u32[]{:S(2)}) %all-to-all-start) | async-done | bytes 1572896 | tf_op jit(solution)/shard_map/all_to_all | solution.py:700
  41.9 0.0 copy-done.6
  41.9 6.5 %spectral.1 = f32[3072,128]{1,0:T(8,128)S(1)} custom-call(f32[3072,128]{1,0:T(8,128)S(1)} %bitcast.14, f32[10752,128]{1,0:T(8,128)} %bitcast.12, f32[896,128]{1,0:T(8,128)S(1)} %bitcast.16, f32[68,128]{1,0:T(8,128)S(1)} %copy-done.7, f32[68,128]{1,0:T(8,128)S(1)} %copy-done.6, bf16[512,256]{1,0:T(8,128)(2,1)S(1)} %copy-done.3, bf16[512,256]{1,0:T(8,128)(2,1)S(1)} %copy-done.2), custom_call_target="tpu_custom_call" | custom-call | tf_op jit(solution)/shard_map/spectral/pallas_call | solution.py:652
  48.4 0.0 copy-start.4
  48.4 0.0 copy-start.8
  48.4 29.5 %all_to_all.10 = f32[128,24,128]{2,1,0:T(8,128)S(1)} all-to-all(f32[128,24,128]{2,1,0:T(8,128)S(1)} %bitcast.15), channel_id=1, replica_groups=mesh['layer'=4,'row'=32] {'layer','row'}, dimensions={0} | all-to-all | bytes 3145728 | tf_op jit(solution)/shard_map/all_to_all | solution.py:700
  78.0 2.0 %inverse_y.1 = f32[192,2048]{1,0:T(8,128)} custom-call(f32[3072,128]{1,0:T(8,128)S(1)} %bitcast.13, bf16[512,256]{1,0:T(8,128)(2,1)S(1)} %copy-done.4, f32[16,128]{1,0:T(8,128)S(1)} %copy-done.8), custom_call_target="tpu_custom_call" | custom-call | tf_op jit(solution)/shard_map/inverse_y/pallas_call | solution.py:682
  (12 shorter events, 0.1 us)
Async XLA Ops:
  0.0 1.4 %copy-start.1 = (f32[3,1,64,2048]{3,2,1,0:T(8,128)S(1)}, f32[3,1,64,2048]{3,2,1,0:T(8,128)}, u32[]{:S(2)}) copy-start(f32[3,1,64,2048]{3,2,1,0:T(8,128)} %param.10) | copy-start | bytes 4718596
  1.4 0.9 %copy-start.5 = (bf16[512,256]{1,0:T(8,128)(2,1)S(1)}, bf16[512,256]{1,0:T(8,128)(2,1)}, u32[]{:S(2)}) copy-start(bf16[512,256]{1,0:T(8,128)(2,1)} %constant.33.clone.table_ref) | copy-start | bytes 786436
  2.4 0.7 copy-start.9
  5.4 36.5 %all-to-all-start = ((f32[128,24,128]{2,1,0:T(8,128)}), f32[128,24,128]{2,1,0:T(8,128)S(1)}, u32[]{:S(2)}, u32[]{:S(2)}) async-start(f32[128,24,128]{2,1,0:T(8,128)} %forward_y.1), calls=%async_computation | async-start | bytes 3145728 | tf_op jit(solution)/shard_map/all_to_all | solution.py:700
  18.9 10.0 %collective-permute-start = (f32[28,2048]{1,0:T(8,128)}, f32[28,2048]{1,0:T(8,128)S(1)}, u32[]{:S(2)}, u32[]{:S(2)}) collective-permute-start(f32[28,2048]{1,0:T(8,128)} %edge_lines.1), channel_id=1, source_target_pairs={{64,0}} | collective-permute-start | bytes 688136 | tf_op jit(solution)/shard_map/ppermute | solution.py:710
  19.5 9.3 %copy-start.10 = (f32[28,2048]{1,0:T(8,128)S(1)}, f32[28,2048]{1,0:T(8,128)}, u32[]{:S(2)}) copy-start(f32[28,2048]{1,0:T(8,128)} %edge_lines.1) | copy-start | bytes 688132
  26.4 2.4 %copy-start = (f32[32,336,128]{2,1,0:T(8,128)}, f32[32,336,128]{2,1,0:T(8,128)S(1)}, u32[]{:S(2)}) copy-start(f32[32,336,128]{2,1,0:T(8,128)S(1)} %relayout.1) | copy-start | bytes 16515076
  28.9 13.0 %copy-start.2 = (bf16[512,256]{1,0:T(8,128)(2,1)S(1)}, bf16[512,256]{1,0:T(8,128)(2,1)}, u32[]{:S(2)}) copy-start(bf16[512,256]{1,0:T(8,128)(2,1)} %constant.38.clone.back_table_ref) | copy-start | bytes 786436
  28.9 13.0 %copy-start.3 = (bf16[512,256]{1,0:T(8,128)(2,1)S(1)}, bf16[512,256]{1,0:T(8,128)(2,1)}, u32[]{:S(2)}) copy-start(bf16[512,256]{1,0:T(8,128)(2,1)} %constant.37.clone.table_ref) | copy-start | bytes 786436
  28.9 13.0 %copy-start.6 = (f32[68,128]{1,0:T(8,128)S(1)}, f32[68,128]{1,0:T(8,128)}, u32[]{:S(2)}) copy-start(f32[68,128]{1,0:T(8,128)} %constant.36.clone.back_twiddle_ref) | copy-start | bytes 104452
  28.9 13.0 %copy-start.7 = (f32[68,128]{1,0:T(8,128)S(1)}, f32[68,128]{1,0:T(8,128)}, u32[]{:S(2)}) copy-start(f32[68,128]{1,0:T(8,128)} %constant.35.clone.twiddle_ref) | copy-start | bytes 104452
  48.4 29.6 %copy-start.4 = (bf16[512,256]{1,0:T(8,128)(2,1)S(1)}, bf16[512,256]{1,0:T(8,128)(2,1)}, u32[]{:S(2)}) copy-start(bf16[512,256]{1,0:T(8,128)(2,1)} %constant.39.clone.table_ref) | copy-start | bytes 786436
  48.4 29.5 %copy-start.8 = (f32[16,128]{1,0:T(8,128)S(1)}, f32[16,128]{1,0:T(8,128)}, u32[]{:S(2)}) copy-start(f32[16,128]{1,0:T(8,128)} %constant.40.clone.twiddle_ref) | copy-start | bytes 24580
